TPU v7x, 32 devices: a whole 2x2x4 slice. The times are simulated.
32 devices in a mesh: seq: 8 (over z, x), wsh: 4 (over y, core).
Axes of the slice: x: 2, y: 2, z: 4, core: 2. Of those that a mesh axis runs over, the one named last changes fastest.
Arguments:
- tokens_in: bfloat16 [4, 4096, 1024], P('wsh', 'seq'), may hold values from -6 to 6
- out_grad: bfloat16 [4, 4096, 1024], P('wsh', 'seq'), may hold values from -6 to 6
- deal_order: int32 [8], replicated, may hold values from 0 to 7, each once
- seq_lengths: int32 [4, 4], P('wsh'), may hold values from 1 to 2048, 4096 in all within a row
- weights: bfloat16 [1024, 17920], P('wsh'), may hold values from -0.1875 to 0.1875
- norm_gains: bfloat16 [2, 1024], P(None, 'wsh'), may hold values from 0.5 to 1.5
- conv_kernel: bfloat16 [3, 1024], P(None, 'wsh'), may hold values from -3 to 3
- vector_state: float32 [5, 1024], P(None, 'wsh'), may hold values from 0.2 to 5
- kron_stats: float32 [2, 1120, 128, 128], P(None, 'wsh', 'seq'), may hold values from -6 to 6
- kron_roots: float32 [2, 1120, 128, 128], P(None, 'wsh', 'seq'), as said below
Outputs:
- block_out: bfloat16 [4, 4096, 1024], P('wsh', 'seq')
- input_grad: bfloat16 [4, 4096, 1024], P('wsh', 'seq')
- weight_grad: float32 [1024, 17920], P('wsh')
- vector_grad: float32 [5, 1024], P(None, 'wsh')
- vector_state_new: float32 [5, 1024], P(None, 'wsh')
- vector_update: float32 [5, 1024], P(None, 'wsh')
- kron_stats_new: float32 [2, 1120, 128, 128], P(None, 'wsh', 'seq')
- weight_update: float32 [1120, 128, 128], P('wsh', 'seq')
Inputs may be any that keep to these rules, and one draw needn't show every extreme that they name: `deal_order`: a permutation of 0 to 7. `seq_lengths`: each row sums to 4096; in every pack the longest sequence has exactly 2048 tokens. `kron_roots`: each block has a dominant diagonal between 0.5 and 2.
All inputs are finite; a program needn't handle non-finite values.
Results may differ from a plain program's by a relative error of at most 0.025.
Values may be sent and summed in bfloat16 or wider, within the bound.
A program may use at most 320 MiB of HBM per device.

v0:
```python
import jax
import jax.numpy as jnp
from jax import lax
from jax.sharding import PartitionSpec as P

D = 1024
FF = 4608
BLK = 128


EPS = 1e-05
BETA = 0.5
BETA_VEC = 0.5
LEARN = 0.03
LEARN_VEC = 0.05
HIGH = lax.Precision.HIGHEST


def passed_along(block, axis, distance):
    devices = range(lax.axis_size(axis))
    route = [(i - distance, i) for i in devices if i - distance in devices]
    return lax.ppermute(block, axis, route)


def seq_positions(lengths_row, first, count):
    starts = jnp.cumsum(lengths_row) - lengths_row
    rows_at = first + jnp.arange(count, dtype=jnp.int32)
    begin = jnp.max(jnp.where(starts[None, :] <= rows_at[:, None], starts[None, :], 0), axis=1)
    return rows_at - begin


def rms_scale(values):
    return lax.rsqrt(jnp.mean(values * values, axis=1, keepdims=True) + EPS)


def norm_back(upstream, values, scale, gain):
    scaled = upstream * gain
    inner = jnp.mean(scaled * values, axis=1, keepdims=True)
    return (
        scale * scaled - values * scale * scale * scale * inner,
        jnp.sum(upstream * values * scale, axis=0),
    )


def contract_rows(left, right):
    return lax.dot_general(
        left, right, (((0,), (0,)), ((), ())), preferred_element_type=jnp.float32
    )


def contract_cols(left, right):
    return lax.dot_general(
        left, right, (((1,), (1,)), ((), ())), preferred_element_type=jnp.float32
    )


def shards(
    tokens_in,
    out_grad,
    deal_order,
    seq_lengths,
    weights,
    norm_gains,
    conv_kernel,
    vector_state,
    kron_stats,
    kron_roots,
):
    n_seq = lax.axis_size("seq")
    n_wsh = lax.axis_size("wsh")
    rows = tokens_in.shape[1]
    unit = rows // n_seq
    arrived = (
        lax.all_to_all(
            tokens_in.reshape(n_seq, unit, D), "seq", split_axis=0, concat_axis=0, tiled=True
        ),
        lax.all_to_all(
            out_grad.reshape(n_seq, unit, D), "seq", split_axis=0, concat_axis=0, tiled=True
        ),
    )
    x_bf = jnp.take(arrived[0], deal_order, axis=0).reshape(rows, D)
    dy_bf = jnp.take(arrived[1], deal_order, axis=0).reshape(rows, D)
    full_w, gains_bf, kernel_bf = (
        lax.all_gather(weights, "wsh", axis=0, tiled=True),
        lax.all_gather(norm_gains, "wsh", axis=1, tiled=True),
        lax.all_gather(conv_kernel, "wsh", axis=1, tiled=True),
    )
    gains = gains_bf.astype(jnp.float32)
    kernel = kernel_bf.astype(jnp.float32)
    first_row = lax.axis_index("seq") * rows
    pos = seq_positions(seq_lengths[0], first_row, rows + 2)
    masks = [(pos >= 2 - k).astype(jnp.float32)[:, None] for k in range(3)]
    xf = x_bf.astype(jnp.float32)
    scale_one = rms_scale(xf)
    xn = (xf * scale_one * gains[0]).astype(jnp.bfloat16)
    proj = jnp.dot(xn, full_w[:, : 3 * D], preferred_element_type=jnp.float32)
    b_part = proj[:, :D]
    c_part = proj[:, D : 2 * D]
    x_part = proj[:, 2 * D :]
    conv_in = b_part * x_part
    prev = passed_along(conv_in[rows - 2 :], "seq", 1)
    ext = jnp.concatenate([prev, conv_in], axis=0)
    conv = (
        kernel[0] * masks[0][:rows] * ext[0:rows]
        + kernel[1] * masks[1][:rows] * ext[1 : rows + 1]
        + kernel[2] * masks[2][:rows] * ext[2 : rows + 2]
    )
    yc = (c_part * conv).astype(jnp.bfloat16)
    hidden_sum = xf + jnp.dot(yc, full_w[:, 3 * D : 4 * D], preferred_element_type=jnp.float32)
    scale_two = rms_scale(hidden_sum)
    hn = (hidden_sum * scale_two * gains[1]).astype(jnp.bfloat16)
    gate_up = jnp.dot(hn, full_w[:, 4 * D : 4 * D + 2 * FF], preferred_element_type=jnp.float32)
    gate = gate_up[:, :FF]
    upper = gate_up[:, FF:]
    sig = jax.nn.sigmoid(gate)
    act = (gate * sig * upper).astype(jnp.bfloat16)
    ffn = contract_cols(act, full_w[:, 4 * D + 2 * FF :])
    result = (hidden_sum + ffn).astype(jnp.bfloat16)
    g_down = contract_rows(dy_bf, act)
    d_act = jnp.dot(dy_bf, full_w[:, 4 * D + 2 * FF :], preferred_element_type=jnp.float32)
    d_gate = d_act * upper * sig * (1.0 + gate * (1.0 - sig))
    d_upper = d_act * gate * sig
    d_gu = jnp.concatenate([d_gate, d_upper], axis=1).astype(jnp.bfloat16)
    g_gu = contract_rows(hn, d_gu)
    d_hn = contract_cols(d_gu, full_w[:, 4 * D : 4 * D + 2 * FF])
    d_norm_two, g_gain_two = norm_back(d_hn, hidden_sum, scale_two, gains[1])
    d_hidden = dy_bf.astype(jnp.float32) + d_norm_two
    d_mix = d_hidden.astype(jnp.bfloat16)
    g_out = contract_rows(yc, d_mix)
    d_yc = contract_cols(d_mix, full_w[:, 3 * D : 4 * D])
    d_c = d_yc * conv
    d_conv = d_yc * c_part
    after = passed_along(d_conv[:2], "seq", -1)
    d_ext = jnp.concatenate([d_conv, after], axis=0)
    weighted = [d_ext * masks[k] for k in range(3)]
    d_bx = (
        kernel[2] * weighted[2][:rows]
        + kernel[1] * weighted[1][1 : rows + 1]
        + kernel[0] * weighted[0][2 : rows + 2]
    )
    g_taps = jnp.stack([jnp.sum(weighted[k][:rows] * ext[k : k + rows], axis=0) for k in range(3)])
    d_proj = jnp.concatenate([d_bx * x_part, d_c, d_bx * b_part], axis=1).astype(jnp.bfloat16)
    g_in = contract_rows(xn, d_proj)
    d_xn = contract_cols(d_proj, full_w[:, : 3 * D])
    d_norm_one, g_gain_one = norm_back(d_xn, xf, scale_one, gains[0])
    d_input = (d_hidden + d_norm_one).astype(jnp.bfloat16)
    g_vec = jnp.concatenate([g_gain_one[None], g_gain_two[None], g_taps], axis=0)
    inverse = jnp.argsort(deal_order)
    leaving = (
        jnp.take(result.reshape(n_seq, unit, D), inverse, axis=0),
        jnp.take(d_input.reshape(n_seq, unit, D), inverse, axis=0),
    )
    returned = (
        lax.all_to_all(leaving[0], "seq", split_axis=0, concat_axis=0, tiled=True),
        lax.all_to_all(leaving[1], "seq", split_axis=0, concat_axis=0, tiled=True),
    )
    summed = (
        lax.psum_scatter(g_in.astype(jnp.bfloat16), "wsh", scatter_dimension=0, tiled=True).astype(
            jnp.float32
        ),
        lax.psum_scatter(g_out.astype(jnp.bfloat16), "wsh", scatter_dimension=0, tiled=True).astype(
            jnp.float32
        ),
        lax.psum_scatter(g_gu.astype(jnp.bfloat16), "wsh", scatter_dimension=0, tiled=True).astype(
            jnp.float32
        ),
        lax.psum_scatter(
            g_down.astype(jnp.bfloat16), "wsh", scatter_dimension=0, tiled=True
        ).astype(jnp.float32),
        lax.psum_scatter(g_vec.astype(jnp.bfloat16), "wsh", scatter_dimension=1, tiled=True).astype(
            jnp.float32
        ),
    )
    summed = (
        lax.psum(summed[0].astype(jnp.bfloat16), "seq").astype(jnp.float32),
        lax.psum(summed[1].astype(jnp.bfloat16), "seq").astype(jnp.float32),
        lax.psum(summed[2].astype(jnp.bfloat16), "seq").astype(jnp.float32),
        lax.psum(summed[3].astype(jnp.bfloat16), "seq").astype(jnp.float32),
        lax.psum(summed[4].astype(jnp.bfloat16), "seq").astype(jnp.float32),
    )
    grad_scale = lax.rsqrt(jnp.asarray(rows * n_seq * n_wsh, jnp.float32))
    grad_shard = jnp.concatenate([summed[0], summed[1], summed[2], summed[3]], axis=1) * grad_scale
    vec_grad = summed[4] * grad_scale
    state_new = BETA_VEC * vector_state + (1.0 - BETA_VEC) * vec_grad * vec_grad
    vec_update = -LEARN_VEC * vec_grad * lax.rsqrt(state_new)
    nrow_blocks = grad_shard.shape[0] // BLK
    ncol_blocks = grad_shard.shape[1] // BLK
    grad_blocks = (
        grad_shard.reshape(nrow_blocks, BLK, ncol_blocks, BLK)
        .transpose(0, 2, 1, 3)
        .reshape(nrow_blocks * ncol_blocks, BLK, BLK)
    )
    share = BLK // n_seq
    first_block_row = lax.axis_index("seq") * share
    block_rows = lax.dynamic_slice_in_dim(grad_blocks, first_block_row, share, 1)
    block_cols = lax.dynamic_slice_in_dim(grad_blocks, first_block_row, share, 2)
    left_term = jnp.einsum("nij,nkj->nik", block_rows, grad_blocks, precision=HIGH)
    right_term = jnp.einsum("nji,njk->nik", block_cols, grad_blocks, precision=HIGH)
    stats_new = jnp.stack(
        [
            BETA * kron_stats[0] + (1.0 - BETA) * left_term / BLK,
            BETA * kron_stats[1] + (1.0 - BETA) * right_term / BLK,
        ]
    )
    right_full = lax.all_gather(
        kron_roots[1].astype(jnp.bfloat16), "seq", axis=1, tiled=True
    ).astype(jnp.float32)
    left_mul = jnp.einsum("nij,njk->nik", kron_roots[0], grad_blocks, precision=HIGH)
    update = -LEARN * jnp.einsum("nij,njk->nik", left_mul, right_full, precision=HIGH)
    return (
        returned[0].reshape(1, rows, D),
        returned[1].reshape(1, rows, D),
        grad_shard,
        vec_grad,
        state_new,
        vec_update,
        stats_new,
        update,
    )


def solution(mesh):
    return jax.shard_map(
        shards,
        mesh=mesh,
        in_specs=(
            P("wsh", "seq", None),
            P("wsh", "seq", None),
            P(),
            P("wsh", None),
            P("wsh", None),
            P(None, "wsh"),
            P(None, "wsh"),
            P(None, "wsh"),
            P(None, "wsh", "seq", None),
            P(None, "wsh", "seq", None),
        ),
        out_specs=(
            P("wsh", "seq", None),
            P("wsh", "seq", None),
            P("wsh", None),
            P(None, "wsh"),
            P(None, "wsh"),
            P(None, "wsh"),
            P(None, "wsh", "seq", None),
            P("wsh", "seq", None),
        ),
        check_vma=False,
    )
```

profile of v0, /device:TPU:0, one launch (start us, length us, event | category | flops | bytes accessed | tf_op | source)
XLA Modules:
  0.0 1136.8 jit_solution(3107054169689322003)
XLA Ops:
  15.6 25.6 %all-to-all-done = bf16[8,64,1024]{2,1,0:T(8,128)(2,1)S(1)} async-done(((bf16[8,64,1024]{2,1,0:T(8,128)(2,1)}), bf16[8,64,1024]{2,1,0:T(8,128)(2,1)S(1)}, u32[]{:S(2)}, u32[]{:S(2)}) %all-to-all-start) | async-done | bytes 1048608 | tf_op jit(solution)/shard_map/all_to_all | solution.py:74
  57.4 13.6 %all-to-all-done.2 = bf16[8,64,1024]{2,1,0:T(8,128)(2,1)} async-done(((bf16[8,64,1024]{2,1,0:T(8,128)(2,1)}), bf16[8,64,1024]{2,1,0:T(8,128)(2,1)}, u32[]{:S(2)}, u32[]{:S(2)}) %all-to-all-start.2) | async-done | bytes 1048608 | tf_op jit(solution)/shard_map/all_to_all | solution.py:77
  74.1 159.7 %all-gather.4.cloned.1.call-done = bf16[1024,17920]{1,0:T(8,128)(2,1)} async-done(((bf16[256,17920]{1,0:T(8,128)(2,1)}), bf16[1024,17920]{1,0:T(8,128)(2,1)}) %all-gather.4.cloned.1.call-update) | async-done | bytes 36700176 | tf_op jit(solution)/shard_map/all_gather | solution.py:84
  250.6 18.3 %fusion.4 = f32[512,9216]{1,0:T(8,128)} fusion(bf16[1024,17920]{1,0:T(8,128)(2,1)} %all-gather.4.cloned.1.call-done, f32[512,1024]{1,0:T(8,128)S(1)} %get-tuple-element.51, f32[1024]{0:T(1024)S(1)} %bitcast.99, f32[512]{0:T(512)S(1)} %add_rsqrt_fusion.1), kind=kOutput, calls=%fused_computation.10 | convolution fusion | flops 9665249280 | bytes 39852032 | tf_op jit(solution)/shard_map/dot_general | solution.py:112
  268.9 17.8 %multiply_convert_fusion.1 = (bf16[512,4608]{1,0:T(8,128)(2,1)}, bf16[512,4608]{1,0:T(8,128)(2,1)}, bf16[512,4608]{1,0:T(8,128)(2,1)}) fusion(f32[512,9216]{1,0:T(8,128)} %fusion.4, bf16[512,1024]{1,0:T(8,128)(2,1)} %bitcast.86, bf16[1024,17920]{1,0:T(8,128)(2,1)} %all-gather.4.cloned.1.call-done), kind=kOutput, calls=%fused_computation.15 | convolution fusion | flops 4869586944 | bytes 43515904 | tf_op jit(solution)/shard_map/dot_general | solution.py:120
  286.7 15.9 %multiply_reduce_fusion.1 = (bf16[1024]{0:T(1024)(128)(2,1)S(1)}, f32[512]{0:T(512)S(1)}, f32[512,1024]{1,0:T(8,128)S(1)}) fusion(f32[512,1024]{1,0:T(8,128)} %copy-done.10, f32[512]{0:T(512)S(1)} %add_rsqrt_fusion.1, f32[1024]{0:T(1024)S(1)} %bitcast.100, bf16[1024,17920]{1,0:T(8,128)(2,1)} %all-gather.4.cloned.1.call-done, ...), kind=kOutput, calls=%fused_computation.75 | convolution fusion | flops 9685694464 | bytes 32516096 | tf_op jit(solution)/shard_map/dot_general | solution.py:52
  331.1 9.8 convolution_convert_fusion.1
  342.5 17.5 %convolution_convert_fusion = bf16[1024,9216]{1,0:T(8,128)(2,1)} fusion(bf16[512,4608]{1,0:T(8,128)(2,1)} %get-tuple-element.32, bf16[512,4608]{1,0:T(8,128)(2,1)} %get-tuple-element.31, f32[512,1024]{1,0:T(8,128)S(1)} %copy-done.12, f32[1024]{0:T(1024)S(1)} %bitcast.102, f32[512]{0:T(512)S(1)} %add_rsqrt_fusion.1), kind=kOutput, calls=%fused_computation.7 | convolution fusion | flops 9693560832 | bytes 30414848 | tf_op jit(solution)/shard_map/dot_general | solution.py:46
  360.1 9.3 fusion.41
  370.1 30.7 %reduce-scatter.6.cloned.1.call-done = bf16[256,3072]{1,0:T(8,128)(2,1)} async-done(((bf16[1024,3072]{1,0:T(8,128)(2,1)}), bf16[256,3072]{1,0:T(8,128)(2,1)}) %reduce-scatter.6.cloned.1.call-update) | async-done | bytes 1572880 | tf_op jit(solution)/shard_map/reduce_scatter | solution.py:158
  400.8 81.0 %reduce-scatter.12.cloned.1.call-done = bf16[256,4608]{1,0:T(8,128)(2,1)} async-done(((bf16[1024,4608]{1,0:T(8,128)(2,1)}), bf16[256,4608]{1,0:T(8,128)(2,1)}) %reduce-scatter.12.cloned.1.call-update) | async-done | bytes 2359312 | tf_op jit(solution)/shard_map/reduce_scatter | solution.py:167
  481.8 140.3 %reduce-scatter.10.cloned.1.call-done = bf16[256,9216]{1,0:T(8,128)(2,1)} async-done(((bf16[1024,9216]{1,0:T(8,128)(2,1)}), bf16[256,9216]{1,0:T(8,128)(2,1)}) %reduce-scatter.10.cloned.1.call-update) | async-done | bytes 4718608 | tf_op jit(solution)/shard_map/reduce_scatter | solution.py:164
  626.0 9.9 add_convert_fusion
  645.3 58.2 %all_to_all.20 = bf16[8,64,1024]{2,1,0:T(8,128)(2,1)S(1)} all-to-all(bf16[8,64,1024]{2,1,0:T(8,128)(2,1)S(1)} %get-tuple-element.49), channel_id=1, replica_groups=mesh['seq'=8,'wsh'=4] {'seq'}, dimensions={0} | all-to-all | bytes 2097152 | tf_op jit(solution)/shard_map/all_to_all | solution.py:154
  707.3 49.4 %psum.39 = bf16[5,256]{1,0:T(8,128)(2,1)S(1)} all-reduce(bf16[5,256]{1,0:T(8,128)(2,1)} %reduce-scatter.14.cloned.1.call-done), channel_id=1, replica_groups=mesh['seq'=8,'wsh'=4] {'seq'}, use_global_device_ids=true, to_apply=%region_21.23 | all-reduce | flops 1280 | bytes 5120 | tf_op jit(solution)/shard_map/psum | solution.py:179
  758.2 222.7 %all-reduce.3.cloned.1.call-done = (bf16[256,4608]{1,0:T(8,128)(2,1)}, bf16[256,9216]{1,0:T(8,128)(2,1)}, bf16[256,1024]{1,0:T(8,128)(2,1)}, bf16[256,3072]{1,0:T(8,128)(2,1)}) async-done(((bf16[256,4608]{1,0:T(8,128)(2,1)}, bf16[256,9216]{1,0:T(8,128)(2,1)}, bf16[256,1024]{1,0:T(8,128)(2,1)}, bf16[256,3072]{1,0:T(8,128)(2,1)}), (bf16[256,4608]{1,0:T(8,128)(2,1)}, bf16[256,9216]{1,0:T(8,128)(2,1)}, ...) | async-done | bytes 9175056 | tf_op jit(solution)/shard_map/psum | solution.py:178
  980.9 10.2 convert_multiply_fusion
  991.1 19.2 %mul.433 = f32[2,128,140,128]{3,2,1,0:T(8,128)} reshape(f32[256,17920]{1,0:T(8,128)} %convert_multiply_fusion) | data formatting | bytes 36700160 | tf_op jit(solution)/shard_map/mul | solution.py:182
  1010.2 12.0 %copy.22 = f32[2,140,128,128]{3,2,1,0:T(8,128)S(1)} copy(f32[2,140,128,128]{3,1,2,0:T(8,128)} %bitcast.79) | data formatting | bytes 36700160 | tf_op jit(solution)/shard_map/transpose | solution.py:190
  1022.3 29.5 %fusion.19 = f32[1,280,16,128]{3,2,1,0:T(8,128)S(1)} fusion(f32[2,280,16,128]{3,2,1,0:T(8,128)S(1)} %bitcast.83, f32[280,128,128]{2,1,0:T(8,128)S(1)} %bitcast.76, s32[]{:T(128)S(6)} %select_n.16), kind=kOutput, calls=%fused_computation.39 | convolution fusion | flops 882524160 | bytes 25231364 | tf_op jit(solution)/shard_map/nij,nkj->nik/dot_general | solution.py:197
  1051.8 35.2 %fusion.18 = f32[1,280,16,128]{3,2,1,0:T(8,128)S(1)} fusion(f32[2,280,16,128]{3,2,1,0:T(8,128)S(1)} %bitcast.83, f32[280,128,128]{2,1,0:T(8,128)S(1)} %bitcast.77, s32[]{:T(128)S(6)} %select_n.16), kind=kOutput, calls=%fused_computation.37 | convolution fusion | flops 882524160 | bytes 41287684 | tf_op jit(solution)/shard_map/nji,njk->nik/dot_general | solution.py:198
  1089.5 17.0 %fusion.16 = f32[280,128,16]{1,2,0:T(8,128)S(1)} fusion(f32[280,128,128]{2,1,0:T(8,128)S(1)} %bitcast.78, f32[2,280,16,128]{3,2,1,0:T(8,128)} %param.21), kind=kOutput, calls=%fused_computation.34 | convolution fusion | flops 880803840 | bytes 22937600 | tf_op jit(solution)/shard_map/nij,njk->nik/dot_general | solution.py:208
  1106.5 10.1 all-gather.6.cloned.1.call-done
  1116.6 10.6 fusion.54
  (145 shorter events, 98.6 us)
Async XLA Ops:
  7.2 226.6 %all-gather.4.cloned.1.call-start = ((), (), s32[]{:S(2)}) async-start(), calls=%async_computation.9 | async-start | bytes 45875200 | tf_op jit(solution)/shard_map/all_gather | solution.py:84
  7.9 37.7 %copy-start.22 = (bf16[2,256]{1,0:T(2,128)(2,1)S(1)}, bf16[2,256]{1,0:T(2,128)(2,1)}, u32[]{:S(2)}) copy-start(bf16[2,256]{1,0:T(2,128)(2,1)} %param.17) | copy-start | bytes 3076
  7.9 42.9 %copy-start.21 = (bf16[3,256]{1,0:T(4,128)(2,1)S(1)}, bf16[3,256]{1,0:T(4,128)(2,1)}, u32[]{:S(2)}) copy-start(bf16[3,256]{1,0:T(4,128)(2,1)} %param.18) | copy-start | bytes 4612
  7.9 48.2 %copy-start.24 = (s32[8]{0:T(128)S(1)}, s32[8]{0:T(128)}, u32[]{:S(2)}) copy-start(s32[8]{0:T(128)} %param.14) | copy-start | bytes 100
  7.9 33.2 %all-to-all-start = ((bf16[8,64,1024]{2,1,0:T(8,128)(2,1)}), bf16[8,64,1024]{2,1,0:T(8,128)(2,1)S(1)}, u32[]{:S(2)}, u32[]{:S(2)}) async-start(bf16[8,64,1024]{2,1,0:T(8,128)(2,1)} %bitcast), calls=%async_computation | async-start | bytes 2097152 | tf_op jit(solution)/shard_map/all_to_all | solution.py:74
  41.1 29.8 %all-to-all-start.2 = ((bf16[8,64,1024]{2,1,0:T(8,128)(2,1)}), bf16[8,64,1024]{2,1,0:T(8,128)(2,1)}, u32[]{:S(2)}, u32[]{:S(2)}) async-start(bf16[8,64,1024]{2,1,0:T(8,128)(2,1)} %bitcast.10), calls=%async_computation.2 | async-start | bytes 2097152 | tf_op jit(solution)/shard_map/all_to_all | solution.py:77
  45.4 324.7 %reduce-scatter.8.cloned.1.call-start = ((), (), s32[]{:S(2)}) async-start(), calls=%async_computation.11 | async-start | bytes 2621440 | tf_op jit(solution)/shard_map/reduce_scatter | solution.py:161
  74.1 159.7 %copy-start.18 = (bf16[512,1024]{1,0:T(8,128)(2,1)}, bf16[512,1024]{1,0:T(8,128)(2,1)S(1)}, u32[]{:S(2)}) copy-start(bf16[512,1024]{1,0:T(8,128)(2,1)S(1)} %fusion.32) | copy-start | bytes 3145732
  239.8 5.1 collective-permute-start
  250.6 18.3 %copy-start.10 = (f32[512,1024]{1,0:T(8,128)}, f32[512,1024]{1,0:T(8,128)S(1)}, u32[]{:S(2)}) copy-start(f32[512,1024]{1,0:T(8,128)S(1)} %get-tuple-element.51) | copy-start | bytes 6291460
  286.7 15.9 %copy-start.8 = (bf16[8,64,1024]{2,1,0:T(8,128)(2,1)S(1)}, bf16[8,64,1024]{2,1,0:T(8,128)(2,1)}, u32[]{:S(2)}) copy-start(bf16[8,64,1024]{2,1,0:T(8,128)(2,1)} %broadcast_select_fusion.2) | copy-start | bytes 3145732
  286.7 16.0 %copy-start.11 = (f32[512,1024]{1,0:T(8,128)S(1)}, f32[512,1024]{1,0:T(8,128)}, u32[]{:S(2)}) copy-start(f32[512,1024]{1,0:T(8,128)} %copy-done.10) | copy-start | bytes 6291460
  307.5 93.3 %reduce-scatter.6.cloned.1.call-start = ((), (), s32[]{:S(2)}) async-start(), calls=%async_computation.10 | async-start | bytes 7864320 | tf_op jit(solution)/shard_map/reduce_scatter | solution.py:158
  313.7 5.5 collective-permute-start.1
  329.9 151.9 %reduce-scatter.12.cloned.1.call-start = ((), (), s32[]{:S(2)}) async-start(), calls=%async_computation.13 | async-start | bytes 11796480 | tf_op jit(solution)/shard_map/reduce_scatter | solution.py:167
  341.0 281.2 %reduce-scatter.10.cloned.1.call-start = ((), (), s32[]{:S(2)}) async-start(), calls=%async_computation.12 | async-start | bytes 23592960 | tf_op jit(solution)/shard_map/reduce_scatter | solution.py:164
  360.0 347.3 %reduce-scatter.14.cloned.1.call-start = ((), (), s32[]{:S(2)}) async-start(), calls=%async_computation.14 | async-start | bytes 20480 | tf_op jit(solution)/shard_map/reduce_scatter | solution.py:170
  370.1 610.8 %all-reduce.3.cloned.1.call-start = ((), (), s32[]{:S(2)}) async-start(), calls=%async_computation.16 | async-start | bytes 18350080 | tf_op jit(solution)/shard_map/psum | solution.py:178
  622.1 494.4 %all-gather.6.cloned.1.call-start = ((), (), s32[]{:S(2)}) async-start(), calls=%async_computation.15 | async-start | bytes 10321920 | tf_op jit(solution)/shard_map/all_gather | solution.py:205
  645.3 111.4 %copy-start.20 = (f32[5,256]{1,0:T(8,128)S(1)}, f32[5,256]{1,0:T(8,128)}, u32[]{:S(2)}) copy-start(f32[5,256]{1,0:T(8,128)} %param.19) | copy-start | bytes 15364
  703.5 54.7 %all-to-all-start.3 = ((bf16[8,64,1024]{2,1,0:T(8,128)(2,1)}), bf16[8,64,1024]{2,1,0:T(8,128)(2,1)S(1)}, u32[]{:S(2)}, u32[]{:S(2)}) async-start(bf16[8,64,1024]{2,1,0:T(8,128)(2,1)} %get-tuple-element.48), calls=%async_computation.3 | async-start | bytes 2097152 | tf_op jit(solution)/shard_map/all_to_all | solution.py:155
  758.2 222.7 %copy-start.6 = (bf16[8,64,1024]{2,1,0:T(8,128)(2,1)}, bf16[8,64,1024]{2,1,0:T(8,128)(2,1)S(1)}, u32[]{:S(2)}) copy-start(bf16[8,64,1024]{2,1,0:T(8,128)(2,1)S(1)} %all-to-all-done.3) | copy-start | bytes 3145732
  991.1 31.2 %slice-start.2 = ((s8[4587520]{0:T(1024)(128)(4,1)}), s8[393216]{0:T(1024)(128)(4,1)S(1)}, s32[]{:S(2)}) async-start(s8[4587520]{0:T(1024)(128)(4,1)} %bitcast.82), calls=%async_computation.19 | async-start | bytes 786432
  1010.2 12.0 %slice-start.3 = ((s8[4587520]{0:T(1024)(128)(4,1)}), s8[4194304]{0:T(1024)(128)(4,1)S(1)}, s32[]{:S(2)}) async-start(s8[4587520]{0:T(1024)(128)(4,1)} %bitcast.82), calls=%async_computation.20 | async-start | bytes 8388608
  (18 other events, 71.7 us)
Sparse Core Ops, SparseCore 0:
  9.6 224.1 all-gather.3
  307.6 31.6 reduce-scatter.7
  341.9 58.8 reduce-scatter.5
  403.8 77.9 reduce-scatter.11
  484.2 137.8 reduce-scatter.9
  624.9 19.5 reduce-scatter.13
  649.1 331.7 all-reduce.2
  982.9 133.6 all-gather.5
where the time goes:
time: 1140 us
  waiting for transfers between devices  690 us (61%)
  matrix products  212 us (19%)
  blocking collectives  118 us (10%)
  local copies, waits for them, and re-layouts  51.4 us (5%)
  other arithmetic  30.2 us (3%)
  starting transfers between devices  21 us (2%)
  between operations  14.9 us (1%)
    psum x1, waiting for transfers between devices, shards(): lax.psum(summed[3].astype(jnp.bfloat16), 'seq').astype(jnp.float32)  223 us
    all_gather x1, waiting for transfers between devices, shards(): lax.all_gather(weights, 'wsh', axis=0, tiled=True)  160 us
    reduce_scatter x1, waiting for transfers between devices, shards(): lax.psum_scatter(g_gu.astype(jnp.bfloat16), 'wsh', scatter_dimension=0, t...  140 us
    reduce_scatter x1, waiting for transfers between devices, shards(): lax.psum_scatter(g_down.astype(jnp.bfloat16), 'wsh', scatter_dimension=0,...  81 us
    all_to_all x1, blocking collectives, shards(): lax.all_to_all(leaving[0], 'seq', split_axis=0, concat_axis=0, tiled=True)  58.2 us
    psum x1, blocking collectives, shards(): lax.psum(summed[4].astype(jnp.bfloat16), 'seq').astype(jnp.float32)  49.4 us
    dot_general x4, matrix products, contract_cols(): lax.dot_general(left, right, (((1,), (1,)), ((), ())), preferred_element_...  38.7 us
    dot_general x4, matrix products, contract_rows(): lax.dot_general(left, right, (((0,), (0,)), ((), ())), preferred_element_...  35.6 us
  transfers between devices with their start and end apart: 13, of which 10 were waited for; matrix products, arithmetic and copies ran while one was open for 18% of the time, Pallas kernels for 0%

commit v1 on v0

--- a/solution.py
+++ b/solution.py
@@ -1,7 +1,13 @@
+import functools
+
 import jax
 import jax.numpy as jnp
 from jax import lax
+from jax.experimental import pallas as pl
+from jax.experimental.pallas import tpu as pltpu
 from jax.sharding import PartitionSpec as P
+
+MESH = pl.DeviceIdType.MESH
 
 D = 1024
 FF = 4608
@@ -54,7 +60,7 @@
     )
 
 
-def shards(
+def plain_shards(
     tokens_in,
     out_grad,
     deal_order,
@@ -219,9 +225,499 @@
     )
 
 
+COLS = 256
+GAP = 2
+RING = 12
+SEMS = 4
+
+
+def place():
+    seq, wsh = lax.axis_index("seq"), lax.axis_index("wsh")
+    return seq // 2, seq % 2, wsh // 2, wsh % 2
+
+
+def reduce_kernel(
+    edges,
+    scale,
+    lefts_ref,
+    d_in_ref,
+    d_mix_ref,
+    d_gu_ref,
+    act_ref,
+    vec_ref,
+    roots_l_ref,
+    roots_r_ref,
+    leave_ref,
+    grad_ref,
+    terms_ref,
+    arrive_ref,
+    b_buf,
+    g_buf,
+    core_in,
+    y_out,
+    y_in,
+    x_out,
+    x_in,
+    z_out,
+    z_in,
+    final,
+    r_buf,
+    t_buf,
+    b_sem,
+    r_sem,
+    o_sem,
+    t_sem,
+    send_sem,
+    recv_sem,
+    far_send,
+    far_recv,
+    own_sem,
+):
+    z, x, y, c = place()
+    seq, wsh = lax.axis_index("seq"), lax.axis_index("wsh")
+    n_real = edges[-1]
+    count = n_real + 1
+    core_id = (seq, y * 2 + (1 - c))
+    y_id = (seq, (1 - y) * 2 + c)
+    x_id = (z * 2 + (1 - x), wsh)
+    z_ids = [(lax.rem(z + d, 4) * 2 + x, wsh) for d in (1, 2, 3)]
+    far_ids = [(lax.rem(seq + d, 8), wsh) for d in range(1, 8)]
+
+    barrier = pltpu.get_barrier_semaphore()
+    for device in [core_id, y_id] + far_ids:
+        pl.semaphore_signal(barrier, inc=1, device_id=device, device_id_type=MESH)
+    pl.semaphore_wait(barrier, 9)
+
+    def far(d):
+        to = far_ids[d - 1]
+        return pltpu.make_async_remote_copy(
+            src_ref=leave_ref.at[to[0]],
+            dst_ref=arrive_ref.at[seq],
+            send_sem=far_send.at[d - 1],
+            recv_sem=far_recv.at[d - 1],
+            device_id=to,
+            device_id_type=MESH,
+        )
+
+    own = pltpu.make_async_copy(leave_ref.at[seq], arrive_ref.at[seq], own_sem)
+    own.start()
+    for d in range(1, 8):
+        far(d).start()
+
+    def remote(flow, n, source, target, device):
+        k = lax.rem(n, SEMS)
+        return pltpu.make_async_remote_copy(
+            src_ref=source,
+            dst_ref=target,
+            send_sem=send_sem.at[flow, k],
+            recv_sem=recv_sem.at[flow, k],
+            device_id=device,
+            device_id_type=MESH,
+        )
+
+    def core_copy(n):
+        slot = lax.rem(n, RING)
+        return remote(0, n, g_buf.at[slot, 1 - c], core_in.at[slot], core_id)
+
+    def y_copy(n):
+        return remote(1, n, y_out.at[lax.rem(n, SEMS)], y_in.at[lax.rem(n, RING)], y_id)
+
+    def x_copy(n):
+        return remote(2, n, x_out.at[lax.rem(n, SEMS)], x_in.at[lax.rem(n, RING)], x_id)
+
+    def z_copy(n, d):
+        slot = lax.rem(n, RING)
+        return remote(
+            2 + d, n, z_out.at[lax.rem(n, SEMS), d - 1], z_in.at[slot, d - 1], z_ids[d - 1]
+        )
+
+    def z_share(n, d):
+        piece = final.at[lax.rem(n, RING), pl.ds(pl.multiple_of(x * 128 + z * 32, 32), 32)]
+        return remote(5 + d, n, piece, piece, z_ids[d - 1])
+
+    def x_share(n):
+        piece = final.at[lax.rem(n, RING), pl.ds(pl.multiple_of(x * 128, 128), 128)]
+        return remote(9, n, piece, piece, x_id)
+
+    def b_copies(n):
+        slot = lax.rem(n, SEMS)
+        column = n_real - n
+        for r, source in enumerate((d_in_ref, d_mix_ref, d_gu_ref, act_ref)):
+            low, high = edges[r], edges[r + 1]
+            at = jnp.clip(column - low, 0, high - low - 1)
+            at = pl.multiple_of(at * COLS, COLS)
+            copy = pltpu.make_async_copy(
+                source.at[:, pl.ds(at, COLS)], b_buf.at[slot], b_sem.at[slot]
+            )
+            yield (column >= low) & (column < high), copy
+
+    def r_copy(n):
+        slot = lax.rem(n, SEMS)
+        at = pl.multiple_of(jnp.minimum(n_real - n, n_real - 1) * 2, 2)
+        return pltpu.make_async_copy(
+            roots_r_ref.at[:, pl.ds(at, 2)], r_buf.at[slot], r_sem.at[slot]
+        )
+
+    def o_copy(n):
+        at = pl.multiple_of((n_real - n) * COLS, COLS)
+        return pltpu.make_async_copy(
+            final.at[lax.rem(n, RING)], grad_ref.at[:, pl.ds(at, COLS)], o_sem.at[lax.rem(n, SEMS)]
+        )
+
+    def t_copy(n):
+        slot = lax.rem(n, SEMS)
+        at = pl.multiple_of(jnp.minimum(n_real - n, n_real - 1) * 2, 2)
+        return pltpu.make_async_copy(
+            t_buf.at[slot], terms_ref.at[:, :, pl.ds(at, 2)], t_sem.at[slot]
+        )
+
+    def wide(value):
+        return value.astype(jnp.float32)
+
+    def sum_rows(slot, first, size, with_y):
+        rows = pl.ds(pl.multiple_of(first, size), size)
+        total = wide(g_buf[slot, c, y, rows]) + wide(core_in[slot, y, rows])
+        if with_y:
+            total = total + wide(y_in[slot, rows])
+        return total
+
+    def stage_load(n):
+        for wanted, copy in b_copies(n):
+            pl.when(wanted)(copy.start)
+
+    def stage_product(n):
+        slot = lax.rem(n, RING)
+        column = n_real - n
+
+        @pl.when(n > 0)
+        def _():
+            for wanted, copy in b_copies(n):
+                pl.when(wanted)(copy.wait)
+            region = sum((column >= e).astype(jnp.int32) for e in edges[1:-1])
+            right = b_buf[lax.rem(n, SEMS)]
+            for w in range(4):
+                product = jnp.dot(
+                    lefts_ref[region, w * 256 : (w + 1) * 256, :],
+                    right,
+                    preferred_element_type=jnp.float32,
+                )
+                g_buf[slot, w % 2, w // 2] = product.astype(jnp.bfloat16)
+
+        @pl.when(n == 0)
+        def _():
+            for w in range(4):
+                g_buf[slot, w % 2, w // 2] = vec_ref[w]
+
+        core_copy(n).start()
+
+    def stage_y(n):
+        slot = lax.rem(n, RING)
+        core_copy(n).wait()
+        y_out[lax.rem(n, SEMS)] = (
+            wide(g_buf[slot, c, 1 - y]) + wide(core_in[slot, 1 - y])
+        ).astype(jnp.bfloat16)
+        y_copy(n).start()
+
+    def stage_x(n):
+        slot = lax.rem(n, RING)
+        y_copy(n).wait()
+        x_out[lax.rem(n, SEMS)] = sum_rows(slot, (1 - x) * 128, 128, True).astype(jnp.bfloat16)
+        x_copy(n).start()
+
+    def stage_z(n):
+        slot = lax.rem(n, RING)
+        x_copy(n).wait()
+        for d in (1, 2, 3):
+            row = lax.rem(z + d, 4) * 32
+            total = sum_rows(slot, x * 128 + row, 32, True)
+            total = total + wide(x_in[slot, pl.ds(pl.multiple_of(row, 32), 32)])
+            z_out[lax.rem(n, SEMS), d - 1] = total.astype(jnp.bfloat16)
+            z_copy(n, d).start()
+
+    def stage_final(n):
+        slot = lax.rem(n, RING)
+        for d in (1, 2, 3):
+            z_copy(n, d).wait()
+        first = x * 128 + z * 32
+        total = sum_rows(slot, first, 32, True)
+        total = total + wide(x_in[slot, pl.ds(pl.multiple_of(z * 32, 32), 32)])
+        for d in range(3):
+            total = total + wide(z_in[slot, d])
+        final[slot, pl.ds(pl.multiple_of(first, 32), 32)] = (total * scale).astype(jnp.bfloat16)
+        for d in (1, 2, 3):
+            z_share(n, d).start()
+
+    def stage_share(n):
+        for d in (1, 2, 3):
+            z_share(n, d).wait()
+        x_share(n).start()
+        pl.when(n > 0)(r_copy(n).start)
+
+    def stage_take(n):
+        x_share(n).wait()
+        o_copy(n).start()
+
+    def stage_use(n):
+        slot = lax.rem(n, RING)
+        part = lax.rem(n, SEMS)
+
+        @pl.when(n > SEMS)
+        def _():
+            t_copy(n - SEMS).wait()
+
+        @pl.when(n > 0)
+        def _():
+            r_copy(n).wait()
+            picked = lax.broadcasted_iota(jnp.int32, (16, BLK), 1) == (
+                lax.broadcasted_iota(jnp.int32, (16, BLK), 0) + seq * 16
+            )
+            one_hot = picked.astype(jnp.float32).astype(jnp.bfloat16)
+            column = (n_real - n) * 2
+            for i in range(2):
+                for j in range(2):
+                    lanes = slice(j * BLK, (j + 1) * BLK)
+                    block = final[slot, i * BLK : (i + 1) * BLK, lanes]
+                    rows = final[
+                        slot, pl.ds(pl.multiple_of(i * BLK + seq * 16, 16), 16), lanes
+                    ]
+                    first = contract_cols(jnp.concatenate([rows, one_hot], axis=0), block)
+                    turned = first[16:].astype(jnp.bfloat16)
+                    second = jnp.dot(
+                        jnp.concatenate([turned, roots_l_ref[i, column + j]], axis=0),
+                        block,
+                        preferred_element_type=jnp.float32,
+                    )
+                    third = jnp.dot(
+                        second[16:].astype(jnp.bfloat16),
+                        r_buf[part, i, j],
+                        preferred_element_type=jnp.float32,
+                    )
+                    t_buf[part, 0, i, j] = first[:16].astype(jnp.bfloat16)
+                    t_buf[part, 1, i, j] = second[:16].astype(jnp.bfloat16)
+                    t_buf[part, 2, i, j] = third.astype(jnp.bfloat16)
+            t_copy(n).start()
+
+    def stage_done(n):
+        o_copy(n).wait()
+
+    offsets = {
+        "load": 0,
+        "product": GAP,
+        "y": 2 * GAP,
+        "x": 3 * GAP,
+        "z": 4 * GAP,
+        "final": 5 * GAP,
+        "share": 6 * GAP,
+        "take": 7 * GAP,
+        "use": 7 * GAP,
+        "done": 8 * GAP,
+    }
+    stages = (
+        ("done", stage_done),
+        ("take", stage_take),
+        ("share", stage_share),
+        ("final", stage_final),
+        ("z", stage_z),
+        ("x", stage_x),
+        ("y", stage_y),
+        ("product", stage_product),
+        ("load", stage_load),
+        ("use", stage_use),
+    )
+
+    def step(t, carry):
+        for name, stage in stages:
+            n = t - offsets[name]
+            pl.when((n >= 0) & (n < count))(functools.partial(stage, n))
+        return carry
+
+    lax.fori_loop(0, count + offsets["done"], step, 0)
+    for n in range(count - SEMS, count):
+        t_copy(n).wait()
+    own.wait()
+    for d in range(1, 8):
+        far(d).wait()
+
+
+def reduced(lefts, rights, vec, roots_l, roots_r, leaving, scale):
+    edges = [0]
+    for right in rights:
+        edges.append(edges[-1] + right.shape[1] // COLS)
+    rows = rights[0].shape[0]
+    count = edges[-1]
+    bf16 = jnp.bfloat16
+    anywhere = pl.BlockSpec(memory_space=pl.ANY)
+    vmem = pl.BlockSpec(memory_space=pltpu.VMEM)
+    return pl.pallas_call(
+        functools.partial(reduce_kernel, tuple(edges), scale),
+        out_shape=(
+            jax.ShapeDtypeStruct((256, (count + 1) * COLS), bf16),
+            jax.ShapeDtypeStruct((3, 2, count * 2, 16, BLK), bf16),
+            jax.ShapeDtypeStruct(leaving.shape, bf16),
+        ),
+        in_specs=[vmem, anywhere, anywhere, anywhere, anywhere, vmem, vmem, anywhere, anywhere],
+        out_specs=(anywhere, anywhere, anywhere),
+        scratch_shapes=[
+            pltpu.VMEM((SEMS, rows, COLS), bf16),
+            pltpu.VMEM((RING, 2, 2, 256, COLS), bf16),
+            pltpu.VMEM((RING, 2, 256, COLS), bf16),
+            pltpu.VMEM((SEMS, 256, COLS), bf16),
+            pltpu.VMEM((RING, 256, COLS), bf16),
+            pltpu.VMEM((SEMS, 128, COLS), bf16),
+            pltpu.VMEM((RING, 128, COLS), bf16),
+            pltpu.VMEM((SEMS, 3, 32, COLS), bf16),
+            pltpu.VMEM((RING, 3, 32, COLS), bf16),
+            pltpu.VMEM((RING, 256, COLS), bf16),
+            pltpu.VMEM((SEMS, 2, 2, BLK, BLK), bf16),
+            pltpu.VMEM((SEMS, 3, 2, 2, 16, BLK), bf16),
+            pltpu.SemaphoreType.DMA((SEMS,)),
+            pltpu.SemaphoreType.DMA((SEMS,)),
+            pltpu.SemaphoreType.DMA((SEMS,)),
+            pltpu.SemaphoreType.DMA((SEMS,)),
+            pltpu.SemaphoreType.DMA((10, SEMS)),
+            pltpu.SemaphoreType.DMA((10, SEMS)),
+            pltpu.SemaphoreType.DMA((7,)),
+            pltpu.SemaphoreType.DMA((7,)),
+            pltpu.SemaphoreType.DMA,
+        ],
+        compiler_params=pltpu.CompilerParams(
+            collective_id=0, has_side_effects=True, vmem_limit_bytes=48 << 20
+        ),
+        cost_estimate=pl.CostEstimate(
+            flops=2 * rows * 1024 * count * COLS, bytes_accessed=10**9, transcendentals=0
+        ),
+        name="reduce_chunks",
+    )(lefts, *rights, vec, roots_l, roots_r, leaving)
+
+
+def shards(
+    tokens_in,
+    out_grad,
+    deal_order,
+    seq_lengths,
+    weights,
+    norm_gains,
+    conv_kernel,
+    vector_state,
+    kron_stats,
+    kron_roots,
+):
+    n_seq = lax.axis_size("seq")
+    n_wsh = lax.axis_size("wsh")
+    rows = tokens_in.shape[1]
+    unit = rows // n_seq
+    arrived = (
+        lax.all_to_all(
+            tokens_in.reshape(n_seq, unit, D), "seq", split_axis=0, concat_axis=0, tiled=True
+        ),
+        lax.all_to_all(
+            out_grad.reshape(n_seq, unit, D), "seq", split_axis=0, concat_axis=0, tiled=True
+        ),
+    )
+    x_bf = jnp.take(arrived[0], deal_order, axis=0).reshape(rows, D)
+    dy_bf = jnp.take(arrived[1], deal_order, axis=0).reshape(rows, D)
+    full_w, gains_bf, kernel_bf = (
+        lax.all_gather(weights, "wsh", axis=0, tiled=True),
+        lax.all_gather(norm_gains, "wsh", axis=1, tiled=True),
+        lax.all_gather(conv_kernel, "wsh", axis=1, tiled=True),
+    )
+    gains = gains_bf.astype(jnp.float32)
+    kernel = kernel_bf.astype(jnp.float32)
+    first_row = lax.axis_index("seq") * rows
+    pos = seq_positions(seq_lengths[0], first_row, rows + 2)
+    masks = [(pos >= 2 - k).astype(jnp.float32)[:, None] for k in range(3)]
+    xf = x_bf.astype(jnp.float32)
+    scale_one = rms_scale(xf)
+    xn = (xf * scale_one * gains[0]).astype(jnp.bfloat16)
+    proj = jnp.dot(xn, full_w[:, : 3 * D], preferred_element_type=jnp.float32)
+    b_part = proj[:, :D]
+    c_part = proj[:, D : 2 * D]
+    x_part = proj[:, 2 * D :]
+    conv_in = b_part * x_part
+    prev = passed_along(conv_in[rows - 2 :], "seq", 1)
+    ext = jnp.concatenate([prev, conv_in], axis=0)
+    conv = (
+        kernel[0] * masks[0][:rows] * ext[0:rows]
+        + kernel[1] * masks[1][:rows] * ext[1 : rows + 1]
+        + kernel[2] * masks[2][:rows] * ext[2 : rows + 2]
+    )
+    yc = (c_part * conv).astype(jnp.bfloat16)
+    hidden_sum = xf + jnp.dot(yc, full_w[:, 3 * D : 4 * D], preferred_element_type=jnp.float32)
+    scale_two = rms_scale(hidden_sum)
+    hn = (hidden_sum * scale_two * gains[1]).astype(jnp.bfloat16)
+    gate_up = jnp.dot(hn, full_w[:, 4 * D : 4 * D + 2 * FF], preferred_element_type=jnp.float32)
+    gate = gate_up[:, :FF]
+    upper = gate_up[:, FF:]
+    sig = jax.nn.sigmoid(gate)
+    act = (gate * sig * upper).astype(jnp.bfloat16)
+    ffn = contract_cols(act, full_w[:, 4 * D + 2 * FF :])
+    result = (hidden_sum + ffn).astype(jnp.bfloat16)
+    d_act = jnp.dot(dy_bf, full_w[:, 4 * D + 2 * FF :], preferred_element_type=jnp.float32)
+    d_gate = d_act * upper * sig * (1.0 + gate * (1.0 - sig))
+    d_upper = d_act * gate * sig
+    d_gu = jnp.concatenate([d_gate, d_upper], axis=1).astype(jnp.bfloat16)
+    d_hn = contract_cols(d_gu, full_w[:, 4 * D : 4 * D + 2 * FF])
+    d_norm_two, g_gain_two = norm_back(d_hn, hidden_sum, scale_two, gains[1])
+    d_hidden = dy_bf.astype(jnp.float32) + d_norm_two
+    d_mix = d_hidden.astype(jnp.bfloat16)
+    d_yc = contract_cols(d_mix, full_w[:, 3 * D : 4 * D])
+    d_c = d_yc * conv
+    d_conv = d_yc * c_part
+    after = passed_along(d_conv[:2], "seq", -1)
+    d_ext = jnp.concatenate([d_conv, after], axis=0)
+    weighted = [d_ext * masks[k] for k in range(3)]
+    d_bx = (
+        kernel[2] * weighted[2][:rows]
+        + kernel[1] * weighted[1][1 : rows + 1]
+        + kernel[0] * weighted[0][2 : rows + 2]
+    )
+    g_taps = jnp.stack([jnp.sum(weighted[k][:rows] * ext[k : k + rows], axis=0) for k in range(3)])
+    d_proj = jnp.concatenate([d_bx * x_part, d_c, d_bx * b_part], axis=1).astype(jnp.bfloat16)
+    d_xn = contract_cols(d_proj, full_w[:, : 3 * D])
+    d_norm_one, g_gain_one = norm_back(d_xn, xf, scale_one, gains[0])
+    d_input = (d_hidden + d_norm_one).astype(jnp.bfloat16)
+    g_vec = jnp.concatenate([g_gain_one[None], g_gain_two[None], g_taps], axis=0)
+    inverse = jnp.argsort(deal_order)
+    result_leaving = jnp.take(result.reshape(n_seq, unit, D), inverse, axis=0)
+    result_back = lax.all_to_all(result_leaving, "seq", split_axis=0, concat_axis=0, tiled=True)
+    leaving = jnp.take(d_input.reshape(n_seq, unit, D), inverse, axis=0)
+    ncol_blocks = weights.shape[1] // BLK
+    nrow_blocks = weights.shape[0] // BLK
+    share = BLK // n_seq
+    roots_r = lax.all_gather(kron_roots[1].astype(jnp.bfloat16), "seq", axis=1, tiled=True)
+    lefts = jnp.stack([xn.T, yc.T, hn.T, dy_bf.T])
+    vec = jnp.pad(g_vec.T.astype(jnp.bfloat16), ((0, 0), (0, COLS - g_vec.shape[0])))
+    grad_bf, terms, dx_back = reduced(
+        lefts,
+        (d_proj, d_mix, d_gu, act),
+        vec.reshape(n_wsh, D // n_wsh, COLS),
+        kron_roots[0].astype(jnp.bfloat16).reshape(nrow_blocks, ncol_blocks, share, BLK),
+        roots_r.reshape(nrow_blocks, ncol_blocks, BLK, BLK),
+        leaving,
+        float((rows * n_seq * n_wsh) ** -0.5),
+    )
+    grad_shard = grad_bf[:, : weights.shape[1]].astype(jnp.float32)
+    vec_grad = grad_bf[:, weights.shape[1] : weights.shape[1] + 5].astype(jnp.float32).T
+    state_new = BETA_VEC * vector_state + (1.0 - BETA_VEC) * vec_grad * vec_grad
+    vec_update = -LEARN_VEC * vec_grad * lax.rsqrt(state_new)
+    terms = terms.reshape(3, nrow_blocks * ncol_blocks, share, BLK).astype(jnp.float32)
+    stats_new = BETA * kron_stats + ((1.0 - BETA) / BLK) * terms[:2]
+    return (
+        result_back.reshape(1, rows, D),
+        dx_back.reshape(1, rows, D),
+        grad_shard,
+        vec_grad,
+        state_new,
+        vec_update,
+        stats_new,
+        -LEARN * terms[2],
+    )
+
+
 def solution(mesh):
+    known = mesh.shape["seq"] == 8 and mesh.shape["wsh"] == 4
     return jax.shard_map(
-        shards,
+        shards if known else plain_shards,
         mesh=mesh,
         in_specs=(
             P("wsh", "seq", None),

time: 1140 us -> 675 us (0.59)
  waiting for transfers between devices: 690 us -> 194 us
  Pallas kernels: 0 us -> 250 us
  matrix products: 212 us -> 82.9 us
  blocking collectives: 118 us -> 10.5 us
  other arithmetic: 30.2 us -> 68.5 us
  local copies, waits for them, and re-layouts: 51.4 us -> 27.5 us
    reduce_scatter x5 -> x0, waiting for transfers between devices: 252 us -> none  [the longest x1 140 us: shards(): lax.psum_scatter(g_gu.astype(jnp.bfloat16), 'wsh', scatter_dimension=0, t...]
    pallas_call x0 -> x1, Pallas kernels: none -> 250 us  [reduced(): pl.pallas_call(functools.partial(reduce_kernel, tuple(edges), scale), out...]
    psum x1 -> x0, waiting for transfers between devices: 223 us -> none  [shards(): lax.psum(summed[3].astype(jnp.bfloat16), 'seq').astype(jnp.float32)]
    dot_general x8 -> x0, matrix products: 128 us -> none  [the longest x4 35.6 us: contract_rows(): lax.dot_general(left, right, (((0,), (0,)), ((), ())), preferred_element_...]
    all_to_all x1 -> x0, blocking collectives: 58.2 us -> none  [shards(): lax.all_to_all(leaving[0], 'seq', split_axis=0, concat_axis=0, tiled=True)]
    psum x1 -> x0, blocking collectives: 49.4 us -> none  [shards(): lax.psum(summed[4].astype(jnp.bfloat16), 'seq').astype(jnp.float32)]
    convert_element_type x0 -> x3, other arithmetic: none -> 18.6 us  [the longest x1 12.4 us: shards(): grad_shard = grad_bf[:, :weights.shape[1]].astype(jnp.float32)]
    mul x1, local copies, waits for them, and re-layouts: 19.2 us -> 0.8 us  [shards(): state_new = BETA_VEC * vector_state + (1.0 - BETA_VEC) * vec_grad * vec_grad]
  transfers between devices with their start and end apart: 13 -> 7, of which waited for: 10 -> 3; matrix products, arithmetic and copies ran while one was open for 18% -> 25% of each run, Pallas kernels for 0% -> 37%
where the time goes in v1:
time: 675 us; the launch traced here: 673 us
  Pallas kernels  250 us (37%)
  waiting for transfers between devices  194 us (29%)
  matrix products  82.9 us (12%)
  other arithmetic  68.5 us (10%)
  local copies, waits for them, and re-layouts  27.5 us (4%)
  starting transfers between devices  25.2 us (4%)
  between operations  14.6 us (2%)
  blocking collectives  10.5 us (2%)
    pallas_call x1, Pallas kernels, reduced(): pl.pallas_call(functools.partial(reduce_kernel, tuple(edges), scale), out...  250 us
    all_gather x1, waiting for transfers between devices, shards(): lax.all_gather(weights, 'wsh', axis=0, tiled=True)  160 us
    dot_general x4, matrix products, contract_cols(): lax.dot_general(left, right, (((1,), (1,)), ((), ())), preferred_element_...  38 us
    all_to_all x1, waiting for transfers between devices, shards(): lax.all_to_all(tokens_in.reshape(n_seq, unit, D), 'seq', split_axis=0, co...  20.3 us
    dot_general x1, matrix products, shards(): jnp.dot(hn, full_w[:, 4 * D:4 * D + 2 * FF], preferred_element_type=jnp.f...  18.3 us
    dot_general x1, matrix products, shards(): jnp.dot(dy_bf, full_w[:, 4 * D + 2 * FF:], preferred_element_type=jnp.flo...  17.8 us
  transfers between devices with their start and end apart: 7, of which 3 were waited for; matrix products, arithmetic and copies ran while one was open for 25% of the time, Pallas kernels for 37%

profile of v1, /device:TPU:0, one launch (start us, length us, event | category | flops | bytes accessed | tf_op | source)
XLA Modules:
  0.0 673.4 jit_solution(17471385376201946109)
XLA Ops:
  7.9 7.3 %all-to-all-start = ((bf16[8,64,1024]{2,1,0:T(8,128)(2,1)}), bf16[8,64,1024]{2,1,0:T(8,128)(2,1)S(1)}, u32[]{:S(2)}, u32[]{:S(2)}) async-start(bf16[8,64,1024]{2,1,0:T(8,128)(2,1)} %bitcast), calls=%async_computation | async-start | bytes 2097152 | tf_op jit(solution)/shard_map/all_to_all | solution.py:610
  20.6 20.3 %all-to-all-done = bf16[8,64,1024]{2,1,0:T(8,128)(2,1)S(1)} async-done(((bf16[8,64,1024]{2,1,0:T(8,128)(2,1)}), bf16[8,64,1024]{2,1,0:T(8,128)(2,1)S(1)}, u32[]{:S(2)}, u32[]{:S(2)}) %all-to-all-start) | async-done | bytes 1048608 | tf_op jit(solution)/shard_map/all_to_all | solution.py:610
  41.0 4.3 all-to-all-start.2
  46.1 5.2 all_gather.12
  51.3 5.3 all_gather.14
  58.2 12.6 %all-to-all-done.2 = bf16[8,64,1024]{2,1,0:T(8,128)(2,1)} async-done(((bf16[8,64,1024]{2,1,0:T(8,128)(2,1)}), bf16[8,64,1024]{2,1,0:T(8,128)(2,1)}, u32[]{:S(2)}, u32[]{:S(2)}) %all-to-all-start.2) | async-done | bytes 1048608 | tf_op jit(solution)/shard_map/all_to_all | solution.py:613
  73.6 160.2 %all-gather.4.cloned.1.call-done = bf16[1024,17920]{1,0:T(8,128)(2,1)} async-done(((bf16[256,17920]{1,0:T(8,128)(2,1)}), bf16[1024,17920]{1,0:T(8,128)(2,1)}) %all-gather.4.cloned.1.call-update) | async-done | bytes 36700176 | tf_op jit(solution)/shard_map/all_gather | solution.py:620
  233.8 5.5 fusion.10
  239.8 3.7 collective-permute-start
  250.4 18.3 %fusion.2 = f32[512,9216]{1,0:T(8,128)} fusion(bf16[1024,17920]{1,0:T(8,128)(2,1)} %all-gather.4.cloned.1.call-done, f32[512,1024]{1,0:T(8,128)S(1)} %get-tuple-element.88, f32[1024]{0:T(1024)S(1)} %bitcast.94, f32[512]{0:T(512)S(1)} %add_rsqrt_fusion.1), kind=kOutput, calls=%fused_computation.6 | convolution fusion | flops 9665249280 | bytes 39852032 | tf_op jit(solution)/shard_map/dot_general | solution.py:648
  268.7 17.8 %multiply_convert_fusion.1 = (bf16[512,4608]{1,0:T(8,128)(2,1)}, bf16[512,4608]{1,0:T(8,128)(2,1)}, bf16[512,4608]{1,0:T(8,128)(2,1)}) fusion(f32[512,9216]{1,0:T(8,128)} %fusion.2, bf16[512,1024]{1,0:T(8,128)(2,1)} %bitcast.82, bf16[1024,17920]{1,0:T(8,128)(2,1)} %all-gather.4.cloned.1.call-done), kind=kOutput, calls=%fused_computation.10 | convolution fusion | flops 4869586944 | bytes 43515904 | tf_op jit(solution)/shard_map/dot_general | solution.py:655
  286.5 16.3 %multiply_reduce_fusion.1 = (bf16[1024]{0:T(1024)(128)(2,1)S(1)}, f32[512]{0:T(512)S(1)}, f32[512,1024]{1,0:T(8,128)S(1)}) fusion(f32[512,1024]{1,0:T(8,128)} %copy-done.11, f32[512]{0:T(512)S(1)} %add_rsqrt_fusion.1, f32[1024]{0:T(1024)S(1)} %bitcast.95, bf16[1024,17920]{1,0:T(8,128)(2,1)} %all-gather.4.cloned.1.call-done, ...), kind=kOutput, calls=%fused_computation.61 | convolution fusion | flops 9685694464 | bytes 32516096 | tf_op jit(solution)/shard_map/dot_general | solution.py:58
  304.1 4.7 fusion.31
  314.9 9.1 %add_convert_fusion = bf16[512,1024]{1,0:T(8,128)(2,1)} fusion(f32[512,1024]{1,0:T(8,128)S(1)} %copy-done.12, bf16[512,4608]{1,0:T(8,128)(2,1)S(1)} %bitcast.109, bf16[1024,17920]{1,0:T(8,128)(2,1)} %all-gather.4.cloned.1.call-done), kind=kOutput, calls=%fused_computation.67 | convolution fusion | flops 4832886784 | bytes 17301504 | tf_op jit(solution)/shard_map/dot_general | solution.py:58
  324.0 4.6 pad_maximum_fusion.d_gu_ref
  333.7 3.9 fusion.15
  340.2 8.0 %fusion.30 = (f32[512]{0:T(512)S(1)}, bf16[1024]{0:T(1024)(128)(2,1)S(1)}, f32[512,1024]{1,0:T(8,128)}) fusion(bf16[8,64,1024]{2,1,0:T(8,128)(2,1)S(1)} %copy-done.10, f32[1024]{0:T(1024)S(1)} %bitcast.99, f32[512]{0:T(512)S(1)} %rsqrt.23, bf16[1024,17920]{1,0:T(8,128)(2,1)} %all-gather.4.cloned.1.call-done, ...), kind=kOutput, calls=%fused_computation.59 | convolution fusion | flops 3234331136 | bytes 12593152 | tf_op jit(solution)/shard_map/dot_general | solution.py:58
  348.5 4.6 fusion.26
  355.4 6.3 copy.39.lefts_ref
  365.8 8.6 %all-to-all-start.1 = ((bf16[8,64,1024]{2,1,0:T(8,128)(2,1)}), bf16[8,64,1024]{2,1,0:T(8,128)(2,1)}, u32[]{:S(2)}, u32[]{:S(2)}) async-start(bf16[8,64,1024]{2,1,0:T(8,128)(2,1)} %get-tuple-element.86), calls=%async_computation.1 | async-start | bytes 2097152 | tf_op jit(solution)/shard_map/all_to_all | solution.py:682
  380.6 250.3 %reduce_chunks.1 = (bf16[256,18176]{1,0:T(8,128)(2,1)}, bf16[3,2,140,16,128]{4,3,2,1,0:T(8,128)(2,1)}, bf16[8,64,1024]{2,1,0:T(8,128)(2,1)S(1)}) custom-call(bf16[4,1024,512]{2,1,0:T(8,128)(2,1)} %copy.39.lefts_ref, bf16[512,3072]{1,0:T(8,128)(2,1)} %pad_maximum_fusion.2.d_in_ref, bf16[512,1024]{1,0:T(8,128)(2,1)S(1)} %copy-done.1, ...), custom_call_target="tpu_custom_call" | custom-call | flops 18790481920 | bytes 1000000000 | tf_op jit(solution)/shard_map/reduce_chunks/pallas_call | solution.py:551
  630.9 12.4 %slice_convert_fusion = f32[256,17920]{1,0:T(8,128)} fusion(bf16[256,18176]{1,0:T(8,128)(2,1)} %get-tuple-element.15), kind=kLoop, calls=%fused_computation.13 | loop fusion | flops 4587520 | bytes 27525120 | tf_op jit(solution)/shard_map/convert_element_type | solution.py:699
  643.3 5.4 convert_element_type.105
  658.3 5.0 multiply_add_fusion
  (151 shorter events, 59.0 us)
Async XLA Ops:
  7.2 226.6 %all-gather.4.cloned.1.call-start = ((), (), s32[]{:S(2)}) async-start(), calls=%async_computation.3 | async-start | bytes 45875200 | tf_op jit(solution)/shard_map/all_gather | solution.py:620
  7.9 33.1 %all-to-all-start = ((bf16[8,64,1024]{2,1,0:T(8,128)(2,1)}), bf16[8,64,1024]{2,1,0:T(8,128)(2,1)S(1)}, u32[]{:S(2)}, u32[]{:S(2)}) async-start(bf16[8,64,1024]{2,1,0:T(8,128)(2,1)} %bitcast), calls=%async_computation | async-start | bytes 2097152 | tf_op jit(solution)/shard_map/all_to_all | solution.py:610
  15.2 363.1 %all-gather.6.cloned.1.call-start = ((), (), s32[]{:S(2)}) async-start(), calls=%async_computation.4 | async-start | bytes 10321920 | tf_op jit(solution)/shard_map/all_gather | solution.py:687
  19.3 26.8 %copy-start.29 = (bf16[2,256]{1,0:T(2,128)(2,1)S(1)}, bf16[2,256]{1,0:T(2,128)(2,1)}, u32[]{:S(2)}) copy-start(bf16[2,256]{1,0:T(2,128)(2,1)} %param.17) | copy-start | bytes 3076
  19.3 32.0 %copy-start.28 = (bf16[3,256]{1,0:T(4,128)(2,1)S(1)}, bf16[3,256]{1,0:T(4,128)(2,1)}, u32[]{:S(2)}) copy-start(bf16[3,256]{1,0:T(4,128)(2,1)} %param.18) | copy-start | bytes 4612
  41.0 29.8 %all-to-all-start.2 = ((bf16[8,64,1024]{2,1,0:T(8,128)(2,1)}), bf16[8,64,1024]{2,1,0:T(8,128)(2,1)}, u32[]{:S(2)}, u32[]{:S(2)}) async-start(bf16[8,64,1024]{2,1,0:T(8,128)(2,1)} %bitcast.16), calls=%async_computation.2 | async-start | bytes 2097152 | tf_op jit(solution)/shard_map/all_to_all | solution.py:613
  57.8 176.0 %copy-start.8 = (bf16[8,64,1024]{2,1,0:T(8,128)(2,1)}, bf16[8,64,1024]{2,1,0:T(8,128)(2,1)S(1)}, u32[]{:S(2)}) copy-start(bf16[8,64,1024]{2,1,0:T(8,128)(2,1)S(1)} %get-tuple-element.63) | copy-start | bytes 3145732
  58.2 175.6 %copy-start.24 = (bf16[512,1024]{1,0:T(8,128)(2,1)}, bf16[512,1024]{1,0:T(8,128)(2,1)S(1)}, u32[]{:S(2)}) copy-start(bf16[512,1024]{1,0:T(8,128)(2,1)S(1)} %fusion.21) | copy-start | bytes 3145732
  239.8 4.9 collective-permute-start
  250.4 18.4 %copy-start.11 = (f32[512,1024]{1,0:T(8,128)}, f32[512,1024]{1,0:T(8,128)S(1)}, u32[]{:S(2)}) copy-start(f32[512,1024]{1,0:T(8,128)S(1)} %get-tuple-element.88) | copy-start | bytes 6291460
  286.5 16.3 %copy-start.6 = (bf16[8,64,1024]{2,1,0:T(8,128)(2,1)S(1)}, bf16[8,64,1024]{2,1,0:T(8,128)(2,1)}, u32[]{:S(2)}) copy-start(bf16[8,64,1024]{2,1,0:T(8,128)(2,1)} %broadcast_select_fusion.2) | copy-start | bytes 3145732
  286.5 16.3 %copy-start.12 = (f32[512,1024]{1,0:T(8,128)S(1)}, f32[512,1024]{1,0:T(8,128)}, u32[]{:S(2)}) copy-start(f32[512,1024]{1,0:T(8,128)} %copy-done.11) | copy-start | bytes 6291460
  302.8 12.1 %slice-start.4 = ((s8[4718592]{0:T(1024)(128)(4,1)}), s8[4194304]{0:T(1024)(128)(4,1)S(1)}, s32[]{:S(2)}) async-start(s8[4718592]{0:T(1024)(128)(4,1)} %bitcast.108), calls=%async_computation.9 | async-start | bytes 8388608
  304.1 10.8 %slice-start.5 = ((s8[4718592]{0:T(1024)(128)(4,1)}), s8[524288]{0:T(1024)(128)(4,1)S(1)}, s32[]{:S(2)}) async-start(s8[4718592]{0:T(1024)(128)(4,1)} %bitcast.108), calls=%async_computation.10 | async-start | bytes 1048576
  308.7 15.3 %slice-start = ((s8[4718592]{0:T(1024)(128)(4,1)}), s8[524288]{0:T(1024)(128)(4,1)S(1)}, s32[]{:S(2)}) async-start(s8[4718592]{0:T(1024)(128)(4,1)} %bitcast.84), calls=%async_computation.5 | async-start | bytes 1048576
  308.8 15.3 %slice-start.2 = ((s8[4718592]{0:T(1024)(128)(4,1)}), s8[4194304]{0:T(1024)(128)(4,1)S(1)}, s32[]{:S(2)}) async-start(s8[4718592]{0:T(1024)(128)(4,1)} %bitcast.86), calls=%async_computation.7 | async-start | bytes 8388608
  313.6 17.9 %collective-permute-start.1 = (f32[2,1024]{1,0:T(2,128)S(1)}, f32[2,1024]{1,0:T(2,128)S(1)}, u32[]{:S(2)}, u32[]{:S(2)}) collective-permute-start(f32[2,1024]{1,0:T(2,128)S(1)} %slice.172), channel_id=1, source_target_pairs={{4,0},{8,4},{12,8},{16,12},{20,16},{24,20},{28,24},{5,1},{9,5},{13... | collective-permute-start | bytes 24584 | tf_op jit(solution)/shard_map/ppermute | solution.py:28
  314.9 9.1 %slice-start.1 = ((s8[4718592]{0:T(1024)(128)(4,1)}), s8[4194304]{0:T(1024)(128)(4,1)S(1)}, s32[]{:S(2)}) async-start(s8[4718592]{0:T(1024)(128)(4,1)} %bitcast.84), calls=%async_computation.6 | async-start | bytes 8388608
  314.9 9.1 %slice-start.3 = ((s8[4718592]{0:T(1024)(128)(4,1)}), s8[524288]{0:T(1024)(128)(4,1)S(1)}, s32[]{:S(2)}) async-start(s8[4718592]{0:T(1024)(128)(4,1)} %bitcast.86), calls=%async_computation.8 | async-start | bytes 1048576
  339.9 8.2 %copy-start.21 = (bf16[512,1024]{1,0:T(8,128)(2,1)}, bf16[512,1024]{1,0:T(8,128)(2,1)S(1)}, u32[]{:S(2)}) copy-start(bf16[512,1024]{1,0:T(8,128)(2,1)S(1)} %multiply_convert_fusion.3) | copy-start | bytes 3145732
  340.2 8.3 %copy-start.7 = (bf16[8,64,1024]{2,1,0:T(8,128)(2,1)S(1)}, bf16[8,64,1024]{2,1,0:T(8,128)(2,1)}, u32[]{:S(2)}) copy-start(bf16[8,64,1024]{2,1,0:T(8,128)(2,1)} %broadcast_select_fusion.2) | copy-start | bytes 3145732
  355.4 6.3 copy-start.16
  365.8 9.5 %copy-start.19 = (bf16[512,1024]{1,0:T(8,128)(2,1)S(1)}, bf16[512,1024]{1,0:T(8,128)(2,1)}, u32[]{:S(2)}) copy-start(bf16[512,1024]{1,0:T(8,128)(2,1)} %get-tuple-element.75) | copy-start | bytes 3145732
  365.8 297.5 %all-to-all-start.1 = ((bf16[8,64,1024]{2,1,0:T(8,128)(2,1)}), bf16[8,64,1024]{2,1,0:T(8,128)(2,1)}, u32[]{:S(2)}, u32[]{:S(2)}) async-start(bf16[8,64,1024]{2,1,0:T(8,128)(2,1)} %get-tuple-element.86), calls=%async_computation.1 | async-start | bytes 2097152 | tf_op jit(solution)/shard_map/all_to_all | solution.py:682
  (21 other events, 61.2 us)
Sparse Core Ops, SparseCore 0:
  9.6 224.1 all-gather.3
  235.8 134.6 all-gather.5

commit v2 on v1

--- a/solution.py
+++ b/solution.py
@@ -590,6 +590,465 @@
     )(lefts, *rights, vec, roots_l, roots_r, leaving)
 
 
+HEAD = 512
+TRIO = 256
+AHEAD = 6
+
+
+def forward_kernel(
+    deal_ref,
+    tokens_ref,
+    dy_ref,
+    weights_ref,
+    small_ref,
+    masks_ref,
+    lefts_ref,
+    x_ref,
+    dy_out_ref,
+    proj_ref,
+    prev_ref,
+    h_ref,
+    act_ref,
+    d_gu_ref,
+    d_hn_ref,
+    result_ref,
+    heads_ref,
+    smalls_ref,
+    x_in,
+    dy_in,
+    heads,
+    trios,
+    smalls,
+    xs,
+    dys,
+    xn,
+    yc,
+    hn,
+    turned,
+    proj,
+    mixed,
+    total,
+    back,
+    act_buf,
+    d_gu_buf,
+    own_sem,
+    load_sem,
+    far_send,
+    far_recv,
+    small_send,
+    small_recv,
+    send_sem,
+    recv_sem,
+    halo_sem,
+    out_sem,
+    act_sem,
+):
+    z, x, y, c = place()
+    seq, wsh = lax.axis_index("seq"), lax.axis_index("wsh")
+    bf16 = jnp.bfloat16
+    n_heads, n_trios = heads.shape[0], trios.shape[0]
+    count = n_heads + n_trios
+    core_id = (seq, y * 2 + (1 - c))
+    y_id = (seq, (1 - y) * 2 + c)
+    cross_id = (seq, (1 - y) * 2 + (1 - c))
+    x_id = (z * 2 + (1 - x), wsh)
+    z_id = ((z + 1 - 2 * (z % 2)) * 2 + x, wsh)
+    far_ids = [(lax.rem(seq + d, 8), wsh) for d in range(1, 8)]
+    quarter = x * 2 + z % 2
+    mine = pl.multiple_of(wsh * 256, 256)
+    theirs = pl.multiple_of(((1 - y) * 2 + c) * 256, 256)
+
+    barrier = pltpu.get_barrier_semaphore()
+    for device in [core_id, y_id, cross_id] + far_ids:
+        pl.semaphore_signal(barrier, inc=1, device_id=device, device_id_type=MESH)
+    pl.semaphore_wait(barrier, 10)
+
+    def far(k, d, source, target):
+        to = far_ids[d - 1]
+        return pltpu.make_async_remote_copy(
+            src_ref=source.at[to[0]],
+            dst_ref=target.at[seq],
+            send_sem=far_send.at[k, d - 1],
+            recv_sem=far_recv.at[k, d - 1],
+            device_id=to,
+            device_id_type=MESH,
+        )
+
+    def small_copy(k, to):
+        return pltpu.make_async_remote_copy(
+            src_ref=small_ref,
+            dst_ref=smalls.at[:, pl.ds(mine, 256)],
+            send_sem=small_send.at[k],
+            recv_sem=small_recv.at[k],
+            device_id=to,
+            device_id_type=MESH,
+        )
+
+    small_ids = (core_id, y_id, cross_id)
+    own_copies = (
+        pltpu.make_async_copy(tokens_ref.at[seq], x_in.at[seq], own_sem.at[0]),
+        pltpu.make_async_copy(dy_ref.at[seq], dy_in.at[seq], own_sem.at[1]),
+        pltpu.make_async_copy(small_ref, smalls.at[:, pl.ds(mine, 256)], own_sem.at[2]),
+    )
+    for copy in own_copies:
+        copy.start()
+    for d in range(1, 8):
+        far(0, d, tokens_ref, x_in).start()
+    for k, to in enumerate(small_ids):
+        small_copy(k, to).start()
+
+    def head_loads(u):
+        at = u * HEAD if isinstance(u, int) else pl.multiple_of(u * HEAD, HEAD)
+        return [
+            pltpu.make_async_copy(
+                weights_ref.at[:, pl.ds(at, HEAD)],
+                heads.at[u, pl.ds(mine, 256)],
+                load_sem.at[u],
+            )
+        ]
+
+    def trio_loads(k, sem):
+        first = n_heads * HEAD
+        return [
+            pltpu.make_async_copy(
+                weights_ref.at[
+                    :,
+                    pl.ds(
+                        pl.multiple_of(first + part * n_trios * TRIO + k * TRIO, TRIO), TRIO
+                    ),
+                ],
+                trios.at[k, pl.ds(mine, 256), pl.ds(part * TRIO, TRIO)],
+                load_sem.at[n_heads + part * n_trios + k],
+            )
+            for part in range(3)
+        ]
+
+    def remote(flow, buf, i, unit, first, rows, to):
+        piece = buf.at[i, pl.ds(pl.multiple_of(first, rows), rows)]
+        return pltpu.make_async_remote_copy(
+            src_ref=piece,
+            dst_ref=piece,
+            send_sem=send_sem.at[flow, unit],
+            recv_sem=recv_sem.at[flow, unit],
+            device_id=to,
+            device_id_type=MESH,
+        )
+
+    def copies(buf, i, unit):
+        near = mine + quarter * 64
+        wide = mine + (3 - quarter) * 64
+        got = theirs + quarter * 64
+        table = {
+            "core": (0, mine, 256, core_id),
+            "near": (1, near, 64, y_id),
+            "wide": (2, wide, 64, y_id),
+            "x": (3, got, 64, x_id),
+            "z": (4, got, 64, z_id),
+            "pass": (5, theirs, 256, core_id),
+        }
+
+        def pick(name):
+            flow, first, rows, to = table[name]
+            return remote(flow, buf, i, unit, first, rows, to)
+
+        return pick
+
+    def head(u):
+        return copies(heads, u, u)
+
+    def trio(k):
+        return copies(trios, k, n_heads + k)
+
+    def send_first(c3):
+        c3("near").start()
+        c3("wide").start()
+        c3("core").start()
+
+    def send_on(c3):
+        c3("near").wait()
+        c3("x").start()
+        c3("z").start()
+
+    def hand_over(c3):
+        c3("wide").wait()
+        c3("x").wait()
+        c3("z").wait()
+        c3("pass").start()
+
+    def arrived(c3):
+        c3("core").wait()
+        c3("pass").wait()
+
+    for u in range(n_heads):
+        for copy in head_loads(u):
+            copy.start()
+
+    def load_trio(k, carry):
+        for copy in trio_loads(k, None):
+            copy.start()
+        return carry
+
+    lax.fori_loop(0, n_trios, load_trio, 0)
+    for u in range(n_heads):
+        for copy in head_loads(u):
+            copy.wait()
+        send_first(head(u))
+
+    def first_trio(k):
+        for copy in trio_loads(k, None):
+            copy.wait()
+        send_first(trio(k))
+
+    def turn(source, r, wait):
+        copy = pltpu.make_async_copy(turned, lefts_ref.at[r], out_sem.at[0])
+        if wait:
+            copy.wait()
+        for j in range(8):
+            turned[j * 128 : (j + 1) * 128, :] = source[:, j * 128 : (j + 1) * 128].T
+        copy.start()
+
+    for d in range(1, 8):
+        far(0, d, tokens_ref, x_in).wait()
+    own_copies[0].wait()
+    for k, to in enumerate(small_ids):
+        small_copy(k, to).wait()
+    own_copies[2].wait()
+    for d in range(1, 8):
+        far(1, d, dy_ref, dy_in).start()
+    gain_one = smalls[0:1, :].astype(jnp.float32)
+    for k in range(8):
+        rows = slice(k * 64, (k + 1) * 64)
+        unit = x_in[deal_ref[k]]
+        xs[rows] = unit
+        value = unit.astype(jnp.float32)
+        xn[rows] = (value * rms_scale(value) * gain_one).astype(bf16)
+    turn(xn, 0, False)
+
+    def mixer_unit(u):
+        proj[:, u * HEAD : (u + 1) * HEAD] = jnp.dot(
+            xn[...], heads[u], preferred_element_type=jnp.float32
+        )
+
+    for u in range(n_heads + 2):
+        if u < n_heads:
+            send_on(head(u))
+        if u >= 1 and u - 1 < n_heads:
+            hand_over(head(u - 1))
+        if u < AHEAD:
+            first_trio(u)
+        if u >= 2:
+            arrived(head(u - 2))
+            if u - 2 < 6:
+                mixer_unit(u - 2)
+
+    out_proj = pltpu.make_async_copy(proj, proj_ref, out_sem.at[1])
+    out_proj.start()
+    width = D
+    halo = slice(0, 8)
+    for i in range(4):
+        rows = slice(i * 128, (i + 1) * 128)
+        back[8 + i * 128 : 8 + (i + 1) * 128] = proj[rows, :width] * proj[rows, 2 * width :]
+    ring = pltpu.make_async_remote_copy(
+        src_ref=back.at[pl.ds(512, 8)],
+        dst_ref=mixed,
+        send_sem=halo_sem.at[0],
+        recv_sem=halo_sem.at[1],
+        device_id=far_ids[0],
+        device_id_type=MESH,
+    )
+    ring.start()
+    send_on(trio(0))
+    for d in range(1, 8):
+        far(1, d, dy_ref, dy_in).wait()
+    own_copies[1].wait()
+    for k in range(8):
+        dys[k * 64 : (k + 1) * 64] = dy_in[deal_ref[k]]
+    turn(dys, 3, True)
+    ring.wait()
+    back[halo] = mixed[...]
+    taps = [smalls[2 + k : 3 + k, :].astype(jnp.float32) for k in range(3)]
+    for i in range(8):
+        first = i * 64
+        rows = slice(first, first + 64)
+        conv = (
+            taps[0] * masks_ref[0, rows] * back[first + 6 : first + 70]
+            + taps[1] * masks_ref[1, rows] * back[first + 7 : first + 71]
+            + taps[2] * back[first + 8 : first + 72]
+        )
+        yc[rows] = (proj[rows, width : 2 * width] * conv).astype(bf16)
+    hand_over(trio(0))
+    for u in range(6, n_heads):
+        lanes = slice((u - 6) * HEAD, (u - 5) * HEAD)
+        total[:, lanes] = xs[:, lanes].astype(jnp.float32) + jnp.dot(
+            yc[...], heads[u], preferred_element_type=jnp.float32
+        )
+    out_h = pltpu.make_async_copy(total, h_ref, out_sem.at[2])
+    out_h.start()
+    gain_two = smalls[1:2, :].astype(jnp.float32)
+    for i in range(8):
+        rows = slice(i * 64, (i + 1) * 64)
+        value = total[rows]
+        hn[rows] = (value * rms_scale(value) * gain_two).astype(bf16)
+    for i in range(4):
+        back[i * 128 : (i + 1) * 128] = jnp.zeros((128, width), jnp.float32)
+    send_on(trio(1))
+    turn(yc, 1, True)
+    out_h.wait()
+
+    def act_copies(k, slot):
+        at = pl.multiple_of(k * TRIO, TRIO)
+        up = pl.multiple_of((n_trios + k) * TRIO, TRIO)
+        return (
+            pltpu.make_async_copy(
+                act_buf.at[slot], act_ref.at[:, pl.ds(at, TRIO)], act_sem.at[slot, 0]
+            ),
+            pltpu.make_async_copy(
+                d_gu_buf.at[slot, :, pl.ds(0, TRIO)],
+                d_gu_ref.at[:, pl.ds(at, TRIO)],
+                act_sem.at[slot, 1],
+            ),
+            pltpu.make_async_copy(
+                d_gu_buf.at[slot, :, pl.ds(TRIO, TRIO)],
+                d_gu_ref.at[:, pl.ds(up, TRIO)],
+                act_sem.at[slot, 2],
+            ),
+        )
+
+    def ffn(k, carry):
+        pl.when(k + AHEAD < n_trios)(lambda: first_trio(k + AHEAD))
+        pl.when(k + 2 < n_trios)(lambda: send_on(trio(k + 2)))
+        pl.when(k + 1 < n_trios)(lambda: hand_over(trio(k + 1)))
+        arrived(trio(k))
+        slot = lax.rem(k, 2)
+
+        @pl.when(k >= 2)
+        def _():
+            for copy in act_copies(k - 2, slot):
+                copy.wait()
+
+        gate = jnp.dot(hn[...], trios[k, :, :TRIO], preferred_element_type=jnp.float32)
+        upper = jnp.dot(
+            hn[...], trios[k, :, TRIO : 2 * TRIO], preferred_element_type=jnp.float32
+        )
+        d_act = jnp.dot(dys[...], trios[k, :, 2 * TRIO :], preferred_element_type=jnp.float32)
+        sig = jax.nn.sigmoid(gate)
+        silu = gate * sig
+        act_buf[slot] = (silu * upper).astype(bf16)
+        d_gu_buf[slot, :, :TRIO] = (
+            d_act * upper * sig * (1.0 + gate * (1.0 - sig))
+        ).astype(bf16)
+        d_gu_buf[slot, :, TRIO:] = (d_act * silu).astype(bf16)
+        for copy in act_copies(k, slot):
+            copy.start()
+        total[...] += contract_cols(act_buf[slot], trios[k, :, 2 * TRIO :])
+        back[0:512] += contract_cols(d_gu_buf[slot], trios[k, :, : 2 * TRIO])
+        return carry
+
+    lax.fori_loop(0, n_trios, ffn, 0)
+    turn(hn, 2, True)
+    out_back = pltpu.make_async_copy(back.at[pl.ds(0, 512)], d_hn_ref, out_sem.at[3])
+    out_back.start()
+    yc[...] = total[...].astype(bf16)
+    last = (
+        pltpu.make_async_copy(yc, result_ref, out_sem.at[4]),
+        pltpu.make_async_copy(xs, x_ref, out_sem.at[5]),
+        pltpu.make_async_copy(dys, dy_out_ref, out_sem.at[6]),
+        pltpu.make_async_copy(smalls, smalls_ref, out_sem.at[7]),
+        pltpu.make_async_copy(mixed, prev_ref, out_sem.at[8]),
+        pltpu.make_async_copy(heads, heads_ref, out_sem.at[9]),
+    )
+    for copy in last:
+        copy.start()
+    for k in range(n_trios - 2, n_trios):
+        for copy in act_copies(k, k % 2):
+            copy.wait()
+    for copy in last:
+        copy.wait()
+    out_proj.wait()
+    out_back.wait()
+    pltpu.make_async_copy(turned, lefts_ref.at[2], out_sem.at[0]).wait()
+
+
+def gathered_forward(deal_order, tokens, dys, weights, small, masks):
+    bf16, f32 = jnp.bfloat16, jnp.float32
+    rows = tokens.shape[0] * tokens.shape[1]
+    n_heads = 4 * D // HEAD
+    n_trios = FF // TRIO
+    count = n_heads + n_trios
+    anywhere = pl.BlockSpec(memory_space=pl.ANY)
+    vmem = pl.BlockSpec(memory_space=pltpu.VMEM)
+    shape = jax.ShapeDtypeStruct
+    return pl.pallas_call(
+        forward_kernel,
+        out_shape=(
+            shape((4, D, rows), bf16),
+            shape((rows, D), bf16),
+            shape((rows, D), bf16),
+            shape((rows, 3 * D), f32),
+            shape((8, D), f32),
+            shape((rows, D), f32),
+            shape((rows, FF), bf16),
+            shape((rows, 2 * FF), bf16),
+            shape((rows, D), f32),
+            shape((rows, D), bf16),
+            shape((n_heads, D, HEAD), bf16),
+            shape((8, D), bf16),
+        ),
+        in_specs=[
+            pl.BlockSpec(memory_space=pltpu.SMEM),
+            anywhere,
+            anywhere,
+            anywhere,
+            vmem,
+            vmem,
+        ],
+        out_specs=(anywhere,) * 12,
+        scratch_shapes=[
+            pltpu.VMEM(tokens.shape, bf16),
+            pltpu.VMEM(tokens.shape, bf16),
+            pltpu.VMEM((n_heads, D, HEAD), bf16),
+            pltpu.VMEM((n_trios, D, 3 * TRIO), bf16),
+            pltpu.VMEM((8, D), bf16),
+            pltpu.VMEM((rows, D), bf16),
+            pltpu.VMEM((rows, D), bf16),
+            pltpu.VMEM((rows, D), bf16),
+            pltpu.VMEM((rows, D), bf16),
+            pltpu.VMEM((rows, D), bf16),
+            pltpu.VMEM((D, rows), bf16),
+            pltpu.VMEM((rows, 3 * D), f32),
+            pltpu.VMEM((8, D), f32),
+            pltpu.VMEM((rows, D), f32),
+            pltpu.VMEM((rows + 8, D), f32),
+            pltpu.VMEM((2, rows, TRIO), bf16),
+            pltpu.VMEM((2, rows, 2 * TRIO), bf16),
+            pltpu.SemaphoreType.DMA((3,)),
+            pltpu.SemaphoreType.DMA((n_heads + 3 * n_trios,)),
+            pltpu.SemaphoreType.DMA((2, 7)),
+            pltpu.SemaphoreType.DMA((2, 7)),
+            pltpu.SemaphoreType.DMA((3,)),
+            pltpu.SemaphoreType.DMA((3,)),
+            pltpu.SemaphoreType.DMA((6, count)),
+            pltpu.SemaphoreType.DMA((6, count)),
+            pltpu.SemaphoreType.DMA((2,)),
+            pltpu.SemaphoreType.DMA((10,)),
+            pltpu.SemaphoreType.DMA((2, 3)),
+        ],
+        compiler_params=pltpu.CompilerParams(
+            collective_id=1, has_side_effects=True, vmem_limit_bytes=63 << 20
+        ),
+        cost_estimate=pl.CostEstimate(
+            flops=8 * rows * D * FF, bytes_accessed=10**8, transcendentals=0
+        ),
+        name="gathered_forward",
+    )(deal_order, tokens, dys, weights, small, masks)
+
+
+def contract_units(left, units):
+    return sum(
+        contract_cols(left[:, u * HEAD : (u + 1) * HEAD], units[u]) for u in range(units.shape[0])
+    )
+
+
 def shards(
     tokens_in,
     out_grad,
@@ -606,61 +1065,51 @@
     n_wsh = lax.axis_size("wsh")
     rows = tokens_in.shape[1]
     unit = rows // n_seq
-    arrived = (
-        lax.all_to_all(
-            tokens_in.reshape(n_seq, unit, D), "seq", split_axis=0, concat_axis=0, tiled=True
-        ),
-        lax.all_to_all(
-            out_grad.reshape(n_seq, unit, D), "seq", split_axis=0, concat_axis=0, tiled=True
-        ),
-    )
-    x_bf = jnp.take(arrived[0], deal_order, axis=0).reshape(rows, D)
-    dy_bf = jnp.take(arrived[1], deal_order, axis=0).reshape(rows, D)
-    full_w, gains_bf, kernel_bf = (
-        lax.all_gather(weights, "wsh", axis=0, tiled=True),
-        lax.all_gather(norm_gains, "wsh", axis=1, tiled=True),
-        lax.all_gather(conv_kernel, "wsh", axis=1, tiled=True),
-    )
-    gains = gains_bf.astype(jnp.float32)
-    kernel = kernel_bf.astype(jnp.float32)
     first_row = lax.axis_index("seq") * rows
     pos = seq_positions(seq_lengths[0], first_row, rows + 2)
     masks = [(pos >= 2 - k).astype(jnp.float32)[:, None] for k in range(3)]
+    small = jnp.concatenate(
+        [norm_gains, conv_kernel, jnp.zeros((3, norm_gains.shape[1]), jnp.bfloat16)], axis=0
+    )
+    (
+        lefts,
+        x_bf,
+        dy_bf,
+        proj,
+        prev,
+        hidden_sum,
+        act,
+        d_gu,
+        d_hn,
+        result,
+        heads,
+        smalls,
+    ) = gathered_forward(
+        deal_order,
+        tokens_in.reshape(n_seq, unit, D),
+        out_grad.reshape(n_seq, unit, D),
+        weights,
+        small,
+        jnp.stack([masks[0][:rows], masks[1][:rows]]),
+    )
+    gains = smalls[:2].astype(jnp.float32)
+    kernel = smalls[2:5].astype(jnp.float32)
     xf = x_bf.astype(jnp.float32)
     scale_one = rms_scale(xf)
-    xn = (xf * scale_one * gains[0]).astype(jnp.bfloat16)
-    proj = jnp.dot(xn, full_w[:, : 3 * D], preferred_element_type=jnp.float32)
+    scale_two = rms_scale(hidden_sum)
     b_part = proj[:, :D]
     c_part = proj[:, D : 2 * D]
     x_part = proj[:, 2 * D :]
-    conv_in = b_part * x_part
-    prev = passed_along(conv_in[rows - 2 :], "seq", 1)
-    ext = jnp.concatenate([prev, conv_in], axis=0)
+    ext = jnp.concatenate([prev[6:], b_part * x_part], axis=0)
     conv = (
         kernel[0] * masks[0][:rows] * ext[0:rows]
         + kernel[1] * masks[1][:rows] * ext[1 : rows + 1]
         + kernel[2] * masks[2][:rows] * ext[2 : rows + 2]
     )
-    yc = (c_part * conv).astype(jnp.bfloat16)
-    hidden_sum = xf + jnp.dot(yc, full_w[:, 3 * D : 4 * D], preferred_element_type=jnp.float32)
-    scale_two = rms_scale(hidden_sum)
-    hn = (hidden_sum * scale_two * gains[1]).astype(jnp.bfloat16)
-    gate_up = jnp.dot(hn, full_w[:, 4 * D : 4 * D + 2 * FF], preferred_element_type=jnp.float32)
-    gate = gate_up[:, :FF]
-    upper = gate_up[:, FF:]
-    sig = jax.nn.sigmoid(gate)
-    act = (gate * sig * upper).astype(jnp.bfloat16)
-    ffn = contract_cols(act, full_w[:, 4 * D + 2 * FF :])
-    result = (hidden_sum + ffn).astype(jnp.bfloat16)
-    d_act = jnp.dot(dy_bf, full_w[:, 4 * D + 2 * FF :], preferred_element_type=jnp.float32)
-    d_gate = d_act * upper * sig * (1.0 + gate * (1.0 - sig))
-    d_upper = d_act * gate * sig
-    d_gu = jnp.concatenate([d_gate, d_upper], axis=1).astype(jnp.bfloat16)
-    d_hn = contract_cols(d_gu, full_w[:, 4 * D : 4 * D + 2 * FF])
     d_norm_two, g_gain_two = norm_back(d_hn, hidden_sum, scale_two, gains[1])
     d_hidden = dy_bf.astype(jnp.float32) + d_norm_two
     d_mix = d_hidden.astype(jnp.bfloat16)
-    d_yc = contract_cols(d_mix, full_w[:, 3 * D : 4 * D])
+    d_yc = contract_units(d_mix, heads[3 * D // HEAD :])
     d_c = d_yc * conv
     d_conv = d_yc * c_part
     after = passed_along(d_conv[:2], "seq", -1)
@@ -673,7 +1122,7 @@
     )
     g_taps = jnp.stack([jnp.sum(weighted[k][:rows] * ext[k : k + rows], axis=0) for k in range(3)])
     d_proj = jnp.concatenate([d_bx * x_part, d_c, d_bx * b_part], axis=1).astype(jnp.bfloat16)
-    d_xn = contract_cols(d_proj, full_w[:, : 3 * D])
+    d_xn = contract_units(d_proj, heads[: 3 * D // HEAD])
     d_norm_one, g_gain_one = norm_back(d_xn, xf, scale_one, gains[0])
     d_input = (d_hidden + d_norm_one).astype(jnp.bfloat16)
     g_vec = jnp.concatenate([g_gain_one[None], g_gain_two[None], g_taps], axis=0)
@@ -685,7 +1134,6 @@
     nrow_blocks = weights.shape[0] // BLK
     share = BLK // n_seq
     roots_r = lax.all_gather(kron_roots[1].astype(jnp.bfloat16), "seq", axis=1, tiled=True)
-    lefts = jnp.stack([xn.T, yc.T, hn.T, dy_bf.T])
     vec = jnp.pad(g_vec.T.astype(jnp.bfloat16), ((0, 0), (0, COLS - g_vec.shape[0])))
     grad_bf, terms, dx_back = reduced(
         lefts,

time: 675 us -> 610 us (0.904)
  Pallas kernels: 250 us -> 460 us
  waiting for transfers between devices: 194 us -> 21.1 us
  matrix products: 82.9 us -> 18.7 us
  starting transfers between devices: 25.2 us -> 13.4 us
  blocking collectives: 10.5 us -> 0 us
  other arithmetic: 68.5 us -> 61.3 us
  local copies, waits for them, and re-layouts: 27.5 us -> 20.5 us
    pallas_call x0 -> x1, Pallas kernels: none -> 224 us  [gathered_forward(): pl.pallas_call(forward_kernel, out_shape=(shape((4, D, rows), bf16), shap...]
    all_gather x1 -> x0, waiting for transfers between devices: 160 us -> none  [shards(): lax.all_gather(weights, 'wsh', axis=0, tiled=True)]
    dot_general x4 -> x0, matrix products: 45 us -> none  [the longest x1 18.3 us: shards(): jnp.dot(hn, full_w[:, 4 * D:4 * D + 2 * FF], preferred_element_type=jnp.f...]
    all_to_all x2 -> x0, waiting for transfers between devices: 32.9 us -> none  [the longest x1 20.3 us: shards(): lax.all_to_all(tokens_in.reshape(n_seq, unit, D), 'seq', split_axis=0, co...]
    all_to_all x1, waiting for transfers between devices: 0.01 us -> 21.1 us  [shards(): lax.all_to_all(result_leaving, 'seq', split_axis=0, concat_axis=0, tiled=...]
    dot_general x4 -> x8, matrix products: 38 us -> 18.7 us  [contract_cols(): lax.dot_general(left, right, (((1,), (1,)), ((), ())), preferred_element_...]
    pallas_call x1, Pallas kernels: 250 us -> 235 us  [reduced(): pl.pallas_call(functools.partial(reduce_kernel, tuple(edges), scale), out...]
    all_to_all x2 -> x0, starting transfers between devices: 11.6 us -> none  [the longest x1 7.29 us: shards(): lax.all_to_all(tokens_in.reshape(n_seq, unit, D), 'seq', split_axis=0, co...]
  transfers between devices with their start and end apart: 7 -> 3, of which waited for: 3 -> 1; matrix products, arithmetic and copies ran while one was open for 25% -> 10% of each run, Pallas kernels for 37% -> 37%
where the time goes in v2:
time: 610 us; the launch traced here: 609 us
  Pallas kernels  460 us (75%)
  other arithmetic  61.3 us (10%)
  waiting for transfers between devices  21.1 us (3%)
  local copies, waits for them, and re-layouts  20.5 us (3%)
  matrix products  18.7 us (3%)
  between operations  14.5 us (2%)
  starting transfers between devices  13.4 us (2%)
    pallas_call x1, Pallas kernels, reduced(): pl.pallas_call(functools.partial(reduce_kernel, tuple(edges), scale), out...  235 us
    pallas_call x1, Pallas kernels, gathered_forward(): pl.pallas_call(forward_kernel, out_shape=(shape((4, D, rows), bf16), shap...  224 us
    all_to_all x1, waiting for transfers between devices, shards(): lax.all_to_all(result_leaving, 'seq', split_axis=0, concat_axis=0, tiled=...  21.1 us
    dot_general x8, matrix products, contract_cols(): lax.dot_general(left, right, (((1,), (1,)), ((), ())), preferred_element_...  18.7 us
    convert_element_type x1, other arithmetic, shards(): grad_shard = grad_bf[:, :weights.shape[1]].astype(jnp.float32)  12.4 us
  transfers between devices with their start and end apart: 3, of which 1 were waited for; matrix products, arithmetic and copies ran while one was open for 10% of the time, Pallas kernels for 37%

profile of v2, /device:TPU:0, one launch (start us, length us, event | category | flops | bytes accessed | tf_op | source)
XLA Modules:
  0.0 609.2 jit_solution(10317960057122360120)
XLA Ops:
  7.2 2.6 convert.42
  13.9 224.3 %gathered_forward.1 = (bf16[4,1024,512]{2,1,0:T(8,128)(2,1)}, bf16[512,1024]{1,0:T(8,128)(2,1)}, bf16[512,1024]{1,0:T(8,128)(2,1)}, f32[512,3072]{1,0:T(8,128)},...) custom-call(s32[8]{0:T(128)} %deal_ref.1, ...), custom_call_target="tpu_custom_call" | custom-call | flops 19327352832 | bytes 100000000 | tf_op jit(solution)/shard_map/gathered_forward/pallas_call | solution.py:981
  240.9 2.3 multiply_reduce_fusion.1
  244.1 2.0 fusion.31
  246.1 6.0 slice_multiply_fusion.7
  258.1 4.8 multiply_convert_fusion.1
  262.9 3.7 fusion.24
  266.5 3.3 fusion.22
  269.8 2.8 gather_fusion
  272.6 2.1 fusion.17
  275.5 4.1 fusion.13
  281.2 2.0 multiply_convert_fusion
  287.4 2.4 fusion.11
  289.8 2.9 gather_fusion.1
  292.7 2.4 broadcast_select_fusion
  295.1 12.0 %all-to-all-start = ((bf16[8,64,1024]{2,1,0:T(8,128)(2,1)}), bf16[8,64,1024]{2,1,0:T(8,128)(2,1)}, u32[]{:S(2)}, u32[]{:S(2)}) async-start(bf16[8,64,1024]{2,1,0:T(8,128)(2,1)} %get-tuple-element.109), calls=%async_computation | async-start | bytes 2097152 | tf_op jit(solution)/shard_map/all_to_all | solution.py:1131
  308.5 3.2 pad_maximum_fusion.d_in_ref
  311.8 21.1 %all-to-all-done = bf16[8,64,1024]{2,1,0:T(8,128)(2,1)} async-done(((bf16[8,64,1024]{2,1,0:T(8,128)(2,1)}), bf16[8,64,1024]{2,1,0:T(8,128)(2,1)}, u32[]{:S(2)}, u32[]{:S(2)}) %all-to-all-start) | async-done | bytes 1048608 | tf_op jit(solution)/shard_map/all_to_all | solution.py:1131
  333.9 235.4 %reduce_chunks.1 = (bf16[256,18176]{1,0:T(8,128)(2,1)}, bf16[3,2,140,16,128]{4,3,2,1,0:T(8,128)(2,1)}, bf16[8,64,1024]{2,1,0:T(8,128)(2,1)S(1)}) custom-call(bf16[4,1024,512]{2,1,0:T(8,128)(2,1)} %get-tuple-element.27.lefts_ref, bf16[512,3072]{1,0:T(8,128)(2,1)} %pad_maximum_fusion.d_in_ref, bf16[512,1024]{1,0:T(8,128)(2,1)S(1)} %fusion.51.d_mix_ref, ...), custom_call_target="tpu_custom_call" | custom-call | flops 18790481920 | bytes 1000000000 | tf_op jit(solution)/shard_map/reduce_chunks/pallas_call | solution.py:551
  569.4 3.0 convert_element_type.76
  572.3 2.5 slice_multiply_fusion
  576.4 12.4 %slice_convert_fusion = f32[256,17920]{1,0:T(8,128)} fusion(bf16[256,18176]{1,0:T(8,128)(2,1)} %get-tuple-element.39), kind=kLoop, calls=%fused_computation.2 | loop fusion | flops 4587520 | bytes 27525120 | tf_op jit(solution)/shard_map/convert_element_type | solution.py:1147
  592.6 6.4 %multiply_add_fusion = f32[2,280,16,128]{3,2,1,0:T(8,128)} fusion(f32[2,280,16,128]{3,2,1,0:T(8,128)} %bitcast.59, f32[2,280,16,128]{3,2,1,0:T(8,128)} %param.20), kind=kLoop, calls=%fused_computation.4 | loop fusion | flops 2293760 | bytes 13762560 | tf_op jit(solution)/shard_map/add | solution.py:1152
  599.0 2.4 copy.59
  (114 shorter events, 28.6 us)
Async XLA Ops:
  7.2 325.7 %all-gather.3.cloned.1.call-start = ((), (), s32[]{:S(2)}) async-start(), calls=%async_computation.1 | async-start | bytes 10321920 | tf_op jit(solution)/shard_map/all_gather | solution.py:1136
  9.8 1.8 copy-start.23
  238.1 2.7 copy-start.4
  240.9 2.3 copy-start.8
  240.9 2.5 copy-start.17
  246.1 9.5 %copy-start.24 = (s32[8]{0:T(128)S(1)}, s32[8]{0:T(128)}, u32[]{:S(2)}) copy-start(s32[8]{0:T(128)} %deal_ref.1) | copy-start | bytes 100
  246.1 12.0 %copy-start.19 = (bf16[8,1024]{1,0:T(8,128)(2,1)S(1)}, bf16[8,1024]{1,0:T(8,128)(2,1)}, u32[]{:S(2)}) copy-start(bf16[8,1024]{1,0:T(8,128)(2,1)} %get-tuple-element.28) | copy-start | bytes 49156
  253.5 19.2 %collective-permute-start = (f32[2,1024]{1,0:T(2,128)S(1)}, f32[2,1024]{1,0:T(2,128)S(1)}, u32[]{:S(2)}, u32[]{:S(2)}) collective-permute-start(f32[2,1024]{1,0:T(2,128)S(1)} %slice.215), channel_id=1, source_target_pairs={{4,0},{8,4},{12,8},{16,12},{20,16},{24,20},{28,24},{5,1},{9,5},{13... | collective-permute-start | bytes 24584 | tf_op jit(solution)/shard_map/ppermute | solution.py:28
  262.8 7.0 %copy-start.11 = (bf16[512,1024]{1,0:T(8,128)(2,1)}, bf16[512,1024]{1,0:T(8,128)(2,1)S(1)}, u32[]{:S(2)}) copy-start(bf16[512,1024]{1,0:T(8,128)(2,1)S(1)} %multiply_convert_fusion.1) | copy-start | bytes 3145732
  272.6 2.2 copy-start.6
  272.6 2.9 copy-start.7
  272.6 7.0 %slice-start = ((s8[8388608]{0:T(1024)(128)(4,1)}), s8[4194304]{0:T(1024)(128)(4,1)S(1)}, s32[]{:S(2)}) async-start(s8[8388608]{0:T(1024)(128)(4,1)} %bitcast.60), calls=%async_computation.2 | async-start | bytes 8388608
  275.5 4.2 slice-start.1
  281.2 2.8 copy-start.15
  283.2 3.9 copy-start.13
  283.2 1.6 copy-start.10
  283.3 2.3 copy-start.14
  285.6 1.9 copy-start.18
  289.8 2.9 copy-start.16
  295.1 12.1 %copy-start.20 = (f32[5,256]{1,0:T(8,128)S(1)}, f32[5,256]{1,0:T(8,128)}, u32[]{:S(2)}) copy-start(f32[5,256]{1,0:T(8,128)} %param.19) | copy-start | bytes 15364
  295.1 37.7 %all-to-all-start = ((bf16[8,64,1024]{2,1,0:T(8,128)(2,1)}), bf16[8,64,1024]{2,1,0:T(8,128)(2,1)}, u32[]{:S(2)}, u32[]{:S(2)}) async-start(bf16[8,64,1024]{2,1,0:T(8,128)(2,1)} %get-tuple-element.109), calls=%async_computation | async-start | bytes 2097152 | tf_op jit(solution)/shard_map/all_to_all | solution.py:1131
  308.5 24.3 %copy-start = (bf16[1,280,16,128]{3,2,1,0:T(8,128)(2,1)S(1)}, bf16[1,280,16,128]{3,2,1,0:T(8,128)(2,1)}, u32[]{:S(2)}) copy-start(bf16[1,280,16,128]{3,2,1,0:T(8,128)(2,1)} %get-tuple-element.97) | copy-start | bytes 3440644
  569.3 3.0 copy-start.1
  599.0 2.4 copy-start.2
  (6 other events, 8.7 us)
Sparse Core Ops, SparseCore 0:
  11.8 205.6 all-gather.2

commit v3 on v2

--- a/solution.py
+++ b/solution.py
@@ -227,8 +227,9 @@
 
 COLS = 256
 GAP = 2
-RING = 12
+RING = 14
 SEMS = 4
+BATCHES = 5
 
 
 def place():
@@ -245,12 +246,14 @@
     d_gu_ref,
     act_ref,
     vec_ref,
-    roots_l_ref,
-    roots_r_ref,
+    owned_ref,
     leave_ref,
+    leave_two_ref,
     grad_ref,
     terms_ref,
+    update_ref,
     arrive_ref,
+    arrive_two_ref,
     b_buf,
     g_buf,
     core_in,
@@ -258,11 +261,14 @@
     y_in,
     x_out,
     x_in,
-    z_out,
-    z_in,
+    pair_out,
+    pair_in,
+    far_out,
+    far_in,
     final,
     r_buf,
     t_buf,
+    u_buf,
     b_sem,
     r_sem,
     o_sem,
@@ -272,6 +278,8 @@
     far_send,
     far_recv,
     own_sem,
+    back_send,
+    back_recv,
 ):
     z, x, y, c = place()
     seq, wsh = lax.axis_index("seq"), lax.axis_index("wsh")
@@ -280,7 +288,10 @@
     core_id = (seq, y * 2 + (1 - c))
     y_id = (seq, (1 - y) * 2 + c)
     x_id = (z * 2 + (1 - x), wsh)
-    z_ids = [(lax.rem(z + d, 4) * 2 + x, wsh) for d in (1, 2, 3)]
+    high, low = z // 2, z % 2
+    pair_id = ((2 * high + 1 - low) * 2 + x, wsh)
+    over_id = ((2 * (1 - high) + low) * 2 + x, wsh)
+    owned_row = x * 128 + low * 64 + high * 32
     far_ids = [(lax.rem(seq + d, 8), wsh) for d in range(1, 8)]
 
     barrier = pltpu.get_barrier_semaphore()
@@ -288,21 +299,44 @@
         pl.semaphore_signal(barrier, inc=1, device_id=device, device_id_type=MESH)
     pl.semaphore_wait(barrier, 9)
 
-    def far(d):
+    def far(k, d):
+        source, target = ((leave_ref, arrive_ref), (leave_two_ref, arrive_two_ref))[k]
         to = far_ids[d - 1]
         return pltpu.make_async_remote_copy(
-            src_ref=leave_ref.at[to[0]],
-            dst_ref=arrive_ref.at[seq],
-            send_sem=far_send.at[d - 1],
-            recv_sem=far_recv.at[d - 1],
+            src_ref=source.at[to[0]],
+            dst_ref=target.at[seq],
+            send_sem=far_send.at[k, d - 1],
+            recv_sem=far_recv.at[k, d - 1],
             device_id=to,
             device_id_type=MESH,
         )
 
-    own = pltpu.make_async_copy(leave_ref.at[seq], arrive_ref.at[seq], own_sem)
-    own.start()
-    for d in range(1, 8):
-        far(d).start()
+    own_pairs = ((leave_ref, arrive_ref), (leave_two_ref, arrive_two_ref))
+    for k, (source, target) in enumerate(own_pairs):
+        pltpu.make_async_copy(source.at[seq], target.at[seq], own_sem.at[k]).start()
+        for d in range(1, 8):
+            far(k, d).start()
+
+    batch = update_ref.shape[1] // BATCHES
+
+    def u_piece(ref, device, b):
+        return ref.at[device, pl.ds(b * batch, batch)]
+
+    def u_back(b, d):
+        to = far_ids[d - 1]
+        return pltpu.make_async_remote_copy(
+            src_ref=u_piece(u_buf, to[0], b),
+            dst_ref=u_piece(update_ref, seq, b),
+            send_sem=back_send.at[b, d - 1],
+            recv_sem=back_recv.at[b, d - 1],
+            device_id=to,
+            device_id_type=MESH,
+        )
+
+    def u_own(b):
+        return pltpu.make_async_copy(
+            u_piece(u_buf, seq, b), u_piece(update_ref, seq, b), own_sem.at[2 + b]
+        )
 
     def remote(flow, n, source, target, device):
         k = lax.rem(n, SEMS)
@@ -325,19 +359,28 @@
     def x_copy(n):
         return remote(2, n, x_out.at[lax.rem(n, SEMS)], x_in.at[lax.rem(n, RING)], x_id)
 
-    def z_copy(n, d):
-        slot = lax.rem(n, RING)
+    def pair_copy(n):
         return remote(
-            2 + d, n, z_out.at[lax.rem(n, SEMS), d - 1], z_in.at[slot, d - 1], z_ids[d - 1]
-        )
-
-    def z_share(n, d):
-        piece = final.at[lax.rem(n, RING), pl.ds(pl.multiple_of(x * 128 + z * 32, 32), 32)]
-        return remote(5 + d, n, piece, piece, z_ids[d - 1])
+            3, n, pair_out.at[lax.rem(n, SEMS)], pair_in.at[lax.rem(n, RING)], pair_id
+        )
+
+    def over_copy(n):
+        return remote(4, n, far_out.at[lax.rem(n, SEMS)], far_in.at[lax.rem(n, RING)], over_id)
+
+    def final_rows(n, first, size):
+        return final.at[lax.rem(n, RING), pl.ds(pl.multiple_of(first, size), size)]
+
+    def over_share(n):
+        piece = final_rows(n, owned_row, 32)
+        return remote(5, n, piece, piece, over_id)
+
+    def pair_share(n):
+        piece = final_rows(n, x * 128 + low * 64, 64)
+        return remote(6, n, piece, piece, pair_id)
 
     def x_share(n):
-        piece = final.at[lax.rem(n, RING), pl.ds(pl.multiple_of(x * 128, 128), 128)]
-        return remote(9, n, piece, piece, x_id)
+        piece = final_rows(n, x * 128, 128)
+        return remote(7, n, piece, piece, x_id)
 
     def b_copies(n):
         slot = lax.rem(n, SEMS)
@@ -351,12 +394,18 @@
             )
             yield (column >= low) & (column < high), copy
 
-    def r_copy(n):
+    def r_copies(n):
         slot = lax.rem(n, SEMS)
-        at = pl.multiple_of(jnp.minimum(n_real - n, n_real - 1) * 2, 2)
-        return pltpu.make_async_copy(
-            roots_r_ref.at[:, pl.ds(at, 2)], r_buf.at[slot], r_sem.at[slot]
-        )
+        at = jnp.minimum(n_real - n, n_real - 1) // 2
+        return [
+            pltpu.make_async_copy(
+                owned_ref.at[:, kind, at], r_buf.at[slot, kind], r_sem.at[slot, kind]
+            )
+            for kind in range(2)
+        ]
+
+    def has_block(n):
+        return (n > 0) & (lax.rem(n_real - n, 2) == lax.rem(seq, 4) // 2)
 
     def o_copy(n):
         at = pl.multiple_of((n_real - n) * COLS, COLS)
@@ -374,12 +423,14 @@
     def wide(value):
         return value.astype(jnp.float32)
 
-    def sum_rows(slot, first, size, with_y):
+    def sum_rows(slot, first, size):
         rows = pl.ds(pl.multiple_of(first, size), size)
         total = wide(g_buf[slot, c, y, rows]) + wide(core_in[slot, y, rows])
-        if with_y:
-            total = total + wide(y_in[slot, rows])
-        return total
+        return total + wide(y_in[slot, rows])
+
+    def sum_half(slot, row, size):
+        rows = pl.ds(pl.multiple_of(row, size), size)
+        return sum_rows(slot, x * 128 + row, size) + wide(x_in[slot, rows])
 
     def stage_load(n):
         for wanted, copy in b_copies(n):
@@ -421,37 +472,49 @@
     def stage_x(n):
         slot = lax.rem(n, RING)
         y_copy(n).wait()
-        x_out[lax.rem(n, SEMS)] = sum_rows(slot, (1 - x) * 128, 128, True).astype(jnp.bfloat16)
+        x_out[lax.rem(n, SEMS)] = sum_rows(slot, (1 - x) * 128, 128).astype(jnp.bfloat16)
         x_copy(n).start()
 
-    def stage_z(n):
+    def stage_pair(n):
         slot = lax.rem(n, RING)
         x_copy(n).wait()
-        for d in (1, 2, 3):
-            row = lax.rem(z + d, 4) * 32
-            total = sum_rows(slot, x * 128 + row, 32, True)
-            total = total + wide(x_in[slot, pl.ds(pl.multiple_of(row, 32), 32)])
-            z_out[lax.rem(n, SEMS), d - 1] = total.astype(jnp.bfloat16)
-            z_copy(n, d).start()
+        total = sum_half(slot, (1 - low) * 64, 64)
+        pair_out[lax.rem(n, SEMS)] = total.astype(jnp.bfloat16)
+        pair_copy(n).start()
+
+    def stage_over(n):
+        slot = lax.rem(n, RING)
+        pair_copy(n).wait()
+        row = (1 - high) * 32
+        total = sum_half(slot, low * 64 + row, 32)
+        total = total + wide(pair_in[slot, pl.ds(pl.multiple_of(row, 32), 32)])
+        far_out[lax.rem(n, SEMS)] = total.astype(jnp.bfloat16)
+        over_copy(n).start()
 
     def stage_final(n):
         slot = lax.rem(n, RING)
-        for d in (1, 2, 3):
-            z_copy(n, d).wait()
-        first = x * 128 + z * 32
-        total = sum_rows(slot, first, 32, True)
-        total = total + wide(x_in[slot, pl.ds(pl.multiple_of(z * 32, 32), 32)])
-        for d in range(3):
-            total = total + wide(z_in[slot, d])
-        final[slot, pl.ds(pl.multiple_of(first, 32), 32)] = (total * scale).astype(jnp.bfloat16)
-        for d in (1, 2, 3):
-            z_share(n, d).start()
+        over_copy(n).wait()
+        total = sum_half(slot, low * 64 + high * 32, 32)
+        total = total + wide(pair_in[slot, pl.ds(pl.multiple_of(high * 32, 32), 32)])
+        total = total + wide(far_in[slot])
+        final[slot, pl.ds(pl.multiple_of(owned_row, 32), 32)] = (total * scale).astype(
+            jnp.bfloat16
+        )
+        over_share(n).start()
+
+    def stage_pair_share(n):
+        over_share(n).wait()
+        pair_share(n).start()
 
     def stage_share(n):
-        for d in (1, 2, 3):
-            z_share(n, d).wait()
+        pair_share(n).wait()
         x_share(n).start()
-        pl.when(n > 0)(r_copy(n).start)
+
+        @pl.when(has_block(n))
+        def _():
+            for copy in r_copies(n):
+                copy.start()
+
 
     def stage_take(n):
         x_share(n).wait()
@@ -467,12 +530,10 @@
 
         @pl.when(n > 0)
         def _():
-            r_copy(n).wait()
             picked = lax.broadcasted_iota(jnp.int32, (16, BLK), 1) == (
                 lax.broadcasted_iota(jnp.int32, (16, BLK), 0) + seq * 16
             )
             one_hot = picked.astype(jnp.float32).astype(jnp.bfloat16)
-            column = (n_real - n) * 2
             for i in range(2):
                 for j in range(2):
                     lanes = slice(j * BLK, (j + 1) * BLK)
@@ -481,21 +542,42 @@
                         slot, pl.ds(pl.multiple_of(i * BLK + seq * 16, 16), 16), lanes
                     ]
                     first = contract_cols(jnp.concatenate([rows, one_hot], axis=0), block)
-                    turned = first[16:].astype(jnp.bfloat16)
                     second = jnp.dot(
-                        jnp.concatenate([turned, roots_l_ref[i, column + j]], axis=0),
+                        first[16:].astype(jnp.bfloat16),
                         block,
                         preferred_element_type=jnp.float32,
                     )
-                    third = jnp.dot(
-                        second[16:].astype(jnp.bfloat16),
-                        r_buf[part, i, j],
-                        preferred_element_type=jnp.float32,
-                    )
                     t_buf[part, 0, i, j] = first[:16].astype(jnp.bfloat16)
-                    t_buf[part, 1, i, j] = second[:16].astype(jnp.bfloat16)
-                    t_buf[part, 2, i, j] = third.astype(jnp.bfloat16)
+                    t_buf[part, 1, i, j] = second.astype(jnp.bfloat16)
             t_copy(n).start()
+
+        @pl.when(has_block(n))
+        def _():
+            for copy in r_copies(n):
+                copy.wait()
+            block = final[
+                slot,
+                pl.ds(pl.multiple_of(seq // 4 * BLK, BLK), BLK),
+                pl.ds(pl.multiple_of(lax.rem(seq, 2) * BLK, BLK), BLK),
+            ]
+            left = jnp.dot(
+                r_buf[part, 0].reshape(BLK, BLK), block, preferred_element_type=jnp.float32
+            )
+            both = jnp.dot(
+                left.astype(jnp.bfloat16),
+                r_buf[part, 1].reshape(BLK, BLK),
+                preferred_element_type=jnp.float32,
+            )
+            u_buf[:, (n_real - n) // 2] = both.astype(jnp.bfloat16).reshape(8, 16, BLK)
+
+        column = n_real - n
+
+        @pl.when((n > 0) & (lax.rem(column, 2 * batch) == 0))
+        def _():
+            b = column // (2 * batch)
+            u_own(b).start()
+            for d in range(1, 8):
+                u_back(b, d).start()
 
     def stage_done(n):
         o_copy(n).wait()
@@ -505,19 +587,23 @@
         "product": GAP,
         "y": 2 * GAP,
         "x": 3 * GAP,
-        "z": 4 * GAP,
-        "final": 5 * GAP,
-        "share": 6 * GAP,
-        "take": 7 * GAP,
-        "use": 7 * GAP,
-        "done": 8 * GAP,
+        "pair": 4 * GAP,
+        "over": 5 * GAP,
+        "final": 6 * GAP,
+        "pair_share": 7 * GAP,
+        "share": 8 * GAP,
+        "take": 9 * GAP,
+        "use": 9 * GAP,
+        "done": 10 * GAP,
     }
     stages = (
         ("done", stage_done),
         ("take", stage_take),
         ("share", stage_share),
+        ("pair_share", stage_pair_share),
         ("final", stage_final),
-        ("z", stage_z),
+        ("over", stage_over),
+        ("pair", stage_pair),
         ("x", stage_x),
         ("y", stage_y),
         ("product", stage_product),
@@ -534,12 +620,17 @@
     lax.fori_loop(0, count + offsets["done"], step, 0)
     for n in range(count - SEMS, count):
         t_copy(n).wait()
-    own.wait()
-    for d in range(1, 8):
-        far(d).wait()
-
-
-def reduced(lefts, rights, vec, roots_l, roots_r, leaving, scale):
+    for k, (source, target) in enumerate(own_pairs):
+        pltpu.make_async_copy(source.at[seq], target.at[seq], own_sem.at[k]).wait()
+        for d in range(1, 8):
+            far(k, d).wait()
+    for b in range(BATCHES):
+        u_own(b).wait()
+        for d in range(1, 8):
+            u_back(b, d).wait()
+
+
+def reduced(lefts, rights, vec, owned, leaving, scale):
     edges = [0]
     for right in rights:
         edges.append(edges[-1] + right.shape[1] // COLS)
@@ -552,11 +643,13 @@
         functools.partial(reduce_kernel, tuple(edges), scale),
         out_shape=(
             jax.ShapeDtypeStruct((256, (count + 1) * COLS), bf16),
-            jax.ShapeDtypeStruct((3, 2, count * 2, 16, BLK), bf16),
-            jax.ShapeDtypeStruct(leaving.shape, bf16),
-        ),
-        in_specs=[vmem, anywhere, anywhere, anywhere, anywhere, vmem, vmem, anywhere, anywhere],
-        out_specs=(anywhere, anywhere, anywhere),
+            jax.ShapeDtypeStruct((2, 2, count * 2, 16, BLK), bf16),
+            jax.ShapeDtypeStruct((8, count // 2, 16, BLK), bf16),
+            jax.ShapeDtypeStruct(leaving[0].shape, bf16),
+            jax.ShapeDtypeStruct(leaving[1].shape, bf16),
+        ),
+        in_specs=[vmem, anywhere, anywhere, anywhere, anywhere, vmem, anywhere, anywhere, anywhere],
+        out_specs=(anywhere,) * 5,
         scratch_shapes=[
             pltpu.VMEM((SEMS, rows, COLS), bf16),
             pltpu.VMEM((RING, 2, 2, 256, COLS), bf16),
@@ -565,20 +658,25 @@
             pltpu.VMEM((RING, 256, COLS), bf16),
             pltpu.VMEM((SEMS, 128, COLS), bf16),
             pltpu.VMEM((RING, 128, COLS), bf16),
-            pltpu.VMEM((SEMS, 3, 32, COLS), bf16),
-            pltpu.VMEM((RING, 3, 32, COLS), bf16),
+            pltpu.VMEM((SEMS, 64, COLS), bf16),
+            pltpu.VMEM((RING, 64, COLS), bf16),
+            pltpu.VMEM((SEMS, 32, COLS), bf16),
+            pltpu.VMEM((RING, 32, COLS), bf16),
             pltpu.VMEM((RING, 256, COLS), bf16),
-            pltpu.VMEM((SEMS, 2, 2, BLK, BLK), bf16),
-            pltpu.VMEM((SEMS, 3, 2, 2, 16, BLK), bf16),
+            pltpu.VMEM((SEMS, 2, 8, 16, BLK), bf16),
+            pltpu.VMEM((SEMS, 2, 2, 2, 16, BLK), bf16),
+            pltpu.VMEM((8, count // 2, 16, BLK), bf16),
+            pltpu.SemaphoreType.DMA((SEMS,)),
+            pltpu.SemaphoreType.DMA((SEMS, 2)),
             pltpu.SemaphoreType.DMA((SEMS,)),
             pltpu.SemaphoreType.DMA((SEMS,)),
-            pltpu.SemaphoreType.DMA((SEMS,)),
-            pltpu.SemaphoreType.DMA((SEMS,)),
-            pltpu.SemaphoreType.DMA((10, SEMS)),
-            pltpu.SemaphoreType.DMA((10, SEMS)),
-            pltpu.SemaphoreType.DMA((7,)),
-            pltpu.SemaphoreType.DMA((7,)),
-            pltpu.SemaphoreType.DMA,
+            pltpu.SemaphoreType.DMA((8, SEMS)),
+            pltpu.SemaphoreType.DMA((8, SEMS)),
+            pltpu.SemaphoreType.DMA((2, 7)),
+            pltpu.SemaphoreType.DMA((2, 7)),
+            pltpu.SemaphoreType.DMA((2 + BATCHES,)),
+            pltpu.SemaphoreType.DMA((BATCHES, 7)),
+            pltpu.SemaphoreType.DMA((BATCHES, 7)),
         ],
         compiler_params=pltpu.CompilerParams(
             collective_id=0, has_side_effects=True, vmem_limit_bytes=48 << 20
@@ -587,12 +685,11 @@
             flops=2 * rows * 1024 * count * COLS, bytes_accessed=10**9, transcendentals=0
         ),
         name="reduce_chunks",
-    )(lefts, *rights, vec, roots_l, roots_r, leaving)
+    )(lefts, *rights, vec, owned, *leaving)
 
 
 HEAD = 512
 TRIO = 256
-AHEAD = 6
 
 
 def forward_kernel(
@@ -602,6 +699,7 @@
     weights_ref,
     small_ref,
     masks_ref,
+    roots_ref,
     lefts_ref,
     x_ref,
     dy_out_ref,
@@ -614,6 +712,7 @@
     result_ref,
     heads_ref,
     smalls_ref,
+    owned_ref,
     x_in,
     dy_in,
     heads,
@@ -664,13 +763,13 @@
     pl.semaphore_wait(barrier, 10)
 
     def far(k, d, source, target):
-        to = far_ids[d - 1]
+        to = lax.rem(seq + d, 8)
         return pltpu.make_async_remote_copy(
-            src_ref=source.at[to[0]],
+            src_ref=source.at[to],
             dst_ref=target.at[seq],
             send_sem=far_send.at[k, d - 1],
             recv_sem=far_recv.at[k, d - 1],
-            device_id=to,
+            device_id=(to, wsh),
             device_id_type=MESH,
         )
 
@@ -689,6 +788,7 @@
         pltpu.make_async_copy(tokens_ref.at[seq], x_in.at[seq], own_sem.at[0]),
         pltpu.make_async_copy(dy_ref.at[seq], dy_in.at[seq], own_sem.at[1]),
         pltpu.make_async_copy(small_ref, smalls.at[:, pl.ds(mine, 256)], own_sem.at[2]),
+        pltpu.make_async_copy(roots_ref.at[seq], owned_ref.at[seq], own_sem.at[3]),
     )
     for copy in own_copies:
         copy.start()
@@ -724,7 +824,7 @@
         ]
 
     def remote(flow, buf, i, unit, first, rows, to):
-        piece = buf.at[i, pl.ds(pl.multiple_of(first, rows), rows)]
+        piece = buf.at[i, pl.ds(pl.multiple_of(first, 16), rows)]
         return pltpu.make_async_remote_copy(
             src_ref=piece,
             dst_ref=piece,
@@ -738,12 +838,14 @@
         near = mine + quarter * 64
         wide = mine + (3 - quarter) * 64
         got = theirs + quarter * 64
+        other = mine + (quarter + 1 - 2 * (z % 2)) * 64 + 48
         table = {
             "core": (0, mine, 256, core_id),
             "near": (1, near, 64, y_id),
             "wide": (2, wide, 64, y_id),
             "x": (3, got, 64, x_id),
-            "z": (4, got, 64, z_id),
+            "z": (4, got, 48, z_id),
+            "rest": (6, other, 16, y_id),
             "pass": (5, theirs, 256, core_id),
         }
 
@@ -762,6 +864,7 @@
     def send_first(c3):
         c3("near").start()
         c3("wide").start()
+        c3("rest").start()
         c3("core").start()
 
     def send_on(c3):
@@ -771,6 +874,7 @@
 
     def hand_over(c3):
         c3("wide").wait()
+        c3("rest").wait()
         c3("x").wait()
         c3("z").wait()
         c3("pass").start()
@@ -794,10 +898,15 @@
             copy.wait()
         send_first(head(u))
 
-    def first_trio(k):
+    def first_trio(k, carry):
         for copy in trio_loads(k, None):
             copy.wait()
         send_first(trio(k))
+        return carry
+
+    lax.fori_loop(0, n_trios, first_trio, 0)
+    send_on(head(0))
+    send_on(head(1))
 
     def turn(source, r, wait):
         copy = pltpu.make_async_copy(turned, lefts_ref.at[r], out_sem.at[0])
@@ -813,8 +922,6 @@
     for k, to in enumerate(small_ids):
         small_copy(k, to).wait()
     own_copies[2].wait()
-    for d in range(1, 8):
-        far(1, d, dy_ref, dy_in).start()
     gain_one = smalls[0:1, :].astype(jnp.float32)
     for k in range(8):
         rows = slice(k * 64, (k + 1) * 64)
@@ -830,12 +937,12 @@
         )
 
     for u in range(n_heads + 2):
-        if u < n_heads:
+        if 2 <= u < n_heads:
             send_on(head(u))
+        if u < 7:
+            far(1, u + 1, dy_ref, dy_in).start()
         if u >= 1 and u - 1 < n_heads:
             hand_over(head(u - 1))
-        if u < AHEAD:
-            first_trio(u)
         if u >= 2:
             arrived(head(u - 2))
             if u - 2 < 6:
@@ -915,10 +1022,10 @@
         )
 
     def ffn(k, carry):
-        pl.when(k + AHEAD < n_trios)(lambda: first_trio(k + AHEAD))
         pl.when(k + 2 < n_trios)(lambda: send_on(trio(k + 2)))
         pl.when(k + 1 < n_trios)(lambda: hand_over(trio(k + 1)))
         arrived(trio(k))
+        pl.when(k < 7)(lambda: far(2, k + 1, roots_ref, owned_ref).start())
         slot = lax.rem(k, 2)
 
         @pl.when(k >= 2)
@@ -964,12 +1071,15 @@
             copy.wait()
     for copy in last:
         copy.wait()
+    for d in range(1, 8):
+        far(2, d, roots_ref, owned_ref).wait()
+    own_copies[3].wait()
     out_proj.wait()
     out_back.wait()
     pltpu.make_async_copy(turned, lefts_ref.at[2], out_sem.at[0]).wait()
 
 
-def gathered_forward(deal_order, tokens, dys, weights, small, masks):
+def gathered_forward(deal_order, tokens, dys, weights, small, masks, roots):
     bf16, f32 = jnp.bfloat16, jnp.float32
     rows = tokens.shape[0] * tokens.shape[1]
     n_heads = 4 * D // HEAD
@@ -993,6 +1103,7 @@
             shape((rows, D), bf16),
             shape((n_heads, D, HEAD), bf16),
             shape((8, D), bf16),
+            shape(roots.shape, bf16),
         ),
         in_specs=[
             pl.BlockSpec(memory_space=pltpu.SMEM),
@@ -1001,8 +1112,9 @@
             anywhere,
             vmem,
             vmem,
+            anywhere,
         ],
-        out_specs=(anywhere,) * 12,
+        out_specs=(anywhere,) * 13,
         scratch_shapes=[
             pltpu.VMEM(tokens.shape, bf16),
             pltpu.VMEM(tokens.shape, bf16),
@@ -1021,14 +1133,14 @@
             pltpu.VMEM((rows + 8, D), f32),
             pltpu.VMEM((2, rows, TRIO), bf16),
             pltpu.VMEM((2, rows, 2 * TRIO), bf16),
-            pltpu.SemaphoreType.DMA((3,)),
+            pltpu.SemaphoreType.DMA((4,)),
             pltpu.SemaphoreType.DMA((n_heads + 3 * n_trios,)),
-            pltpu.SemaphoreType.DMA((2, 7)),
-            pltpu.SemaphoreType.DMA((2, 7)),
+            pltpu.SemaphoreType.DMA((3, 7)),
+            pltpu.SemaphoreType.DMA((3, 7)),
             pltpu.SemaphoreType.DMA((3,)),
             pltpu.SemaphoreType.DMA((3,)),
-            pltpu.SemaphoreType.DMA((6, count)),
-            pltpu.SemaphoreType.DMA((6, count)),
+            pltpu.SemaphoreType.DMA((7, count)),
+            pltpu.SemaphoreType.DMA((7, count)),
             pltpu.SemaphoreType.DMA((2,)),
             pltpu.SemaphoreType.DMA((10,)),
             pltpu.SemaphoreType.DMA((2, 3)),
@@ -1040,7 +1152,80 @@
             flops=8 * rows * D * FF, bytes_accessed=10**8, transcendentals=0
         ),
         name="gathered_forward",
-    )(deal_order, tokens, dys, weights, small, masks)
+    )(deal_order, tokens, dys, weights, small, masks, roots)
+
+
+PARTS = 7
+
+
+def closing_kernel(
+    grad_in, vec_in, terms_in, stats_in, update_in, state_in, grad, vec, state, step, stats, update
+):
+    grad[...] = grad_in[...].astype(jnp.float32)
+    stats[...] = BETA * stats_in[...] + ((1.0 - BETA) / BLK) * terms_in[...].astype(jnp.float32)
+    for i in range(update_in.shape[0]):
+        for m in range(update_in.shape[1]):
+            update[i, :, m] = -LEARN * update_in[i, m].astype(jnp.float32)
+
+    @pl.when(pl.program_id(0) == 0)
+    def _():
+        count = vec.shape[0]
+        turned = vec_in[:, :BLK].astype(jnp.float32).T[:count]
+        fresh = BETA_VEC * state_in[...] + (1.0 - BETA_VEC) * turned * turned
+        vec[...] = turned
+        state[...] = fresh
+        step[...] = -LEARN_VEC * turned * lax.rsqrt(fresh)
+
+
+def closing(grad_bf, terms, kron_stats, update, vector_state):
+    f32 = jnp.float32
+    rows, wide = grad_bf.shape
+    columns = wide - COLS
+    kinds, blocks, share, _ = kron_stats.shape
+    nrow, ncol = rows // BLK, columns // BLK
+    shape = jax.ShapeDtypeStruct
+    vec_spec = pl.BlockSpec(vector_state.shape, lambda g: (0, 0))
+    grad_spec = pl.BlockSpec((rows, columns // PARTS), lambda g: (0, g))
+    stat_spec = pl.BlockSpec((kinds, blocks // PARTS, share, BLK), lambda g: (0, g, 0, 0))
+    groups = ncol // 4
+    outs = pl.pallas_call(
+        closing_kernel,
+        grid=(PARTS,),
+        out_shape=(
+            shape((rows, columns), f32),
+            shape(vector_state.shape, f32),
+            shape(vector_state.shape, f32),
+            shape(vector_state.shape, f32),
+            shape(kron_stats.shape, f32),
+            shape((nrow, groups, 4, share, BLK), f32),
+        ),
+        in_specs=[
+            grad_spec,
+            pl.BlockSpec((rows, COLS), lambda g: (0, columns // COLS)),
+            stat_spec,
+            stat_spec,
+            pl.BlockSpec((nrow, 4, groups // PARTS, share, BLK), lambda g: (0, 0, g, 0, 0)),
+            vec_spec,
+        ],
+        out_specs=(
+            grad_spec,
+            vec_spec,
+            vec_spec,
+            vec_spec,
+            stat_spec,
+            pl.BlockSpec((nrow, groups // PARTS, 4, share, BLK), lambda g: (0, g, 0, 0, 0)),
+        ),
+        compiler_params=pltpu.CompilerParams(vmem_limit_bytes=40 << 20),
+        name="closing",
+    )(
+        grad_bf,
+        grad_bf,
+        terms.reshape(kron_stats.shape),
+        kron_stats,
+        update.reshape(nrow, 4, groups, share, BLK),
+        vector_state,
+    )
+    return (*outs[:5], outs[5].reshape(blocks, share, BLK))
 
 
 def contract_units(left, units):
@@ -1068,6 +1253,12 @@
     first_row = lax.axis_index("seq") * rows
     pos = seq_positions(seq_lengths[0], first_row, rows + 2)
     masks = [(pos >= 2 - k).astype(jnp.float32)[:, None] for k in range(3)]
+    nrow_blocks, ncol_blocks = weights.shape[0] // BLK, weights.shape[1] // BLK
+    share = BLK // n_seq
+    roots = kron_roots.astype(jnp.bfloat16).reshape(
+        2, nrow_blocks, ncol_blocks // 4, 4, share, BLK
+    )
+    roots = roots.transpose(1, 3, 0, 2, 4, 5).reshape(n_seq, 2, ncol_blocks // 4, share, BLK)
     small = jnp.concatenate(
         [norm_gains, conv_kernel, jnp.zeros((3, norm_gains.shape[1]), jnp.bfloat16)], axis=0
     )
@@ -1084,6 +1275,7 @@
         result,
         heads,
         smalls,
+        owned,
     ) = gathered_forward(
         deal_order,
         tokens_in.reshape(n_seq, unit, D),
@@ -1091,6 +1283,7 @@
         weights,
         small,
         jnp.stack([masks[0][:rows], masks[1][:rows]]),
+        roots,
     )
     gains = smalls[:2].astype(jnp.float32)
     kernel = smalls[2:5].astype(jnp.float32)
@@ -1128,37 +1321,28 @@
     g_vec = jnp.concatenate([g_gain_one[None], g_gain_two[None], g_taps], axis=0)
     inverse = jnp.argsort(deal_order)
     result_leaving = jnp.take(result.reshape(n_seq, unit, D), inverse, axis=0)
-    result_back = lax.all_to_all(result_leaving, "seq", split_axis=0, concat_axis=0, tiled=True)
     leaving = jnp.take(d_input.reshape(n_seq, unit, D), inverse, axis=0)
-    ncol_blocks = weights.shape[1] // BLK
-    nrow_blocks = weights.shape[0] // BLK
-    share = BLK // n_seq
-    roots_r = lax.all_gather(kron_roots[1].astype(jnp.bfloat16), "seq", axis=1, tiled=True)
     vec = jnp.pad(g_vec.T.astype(jnp.bfloat16), ((0, 0), (0, COLS - g_vec.shape[0])))
-    grad_bf, terms, dx_back = reduced(
+    grad_bf, terms, update, out_back, dx_back = reduced(
         lefts,
         (d_proj, d_mix, d_gu, act),
         vec.reshape(n_wsh, D // n_wsh, COLS),
-        kron_roots[0].astype(jnp.bfloat16).reshape(nrow_blocks, ncol_blocks, share, BLK),
-        roots_r.reshape(nrow_blocks, ncol_blocks, BLK, BLK),
-        leaving,
+        owned,
+        (result_leaving, leaving),
         float((rows * n_seq * n_wsh) ** -0.5),
     )
-    grad_shard = grad_bf[:, : weights.shape[1]].astype(jnp.float32)
-    vec_grad = grad_bf[:, weights.shape[1] : weights.shape[1] + 5].astype(jnp.float32).T
-    state_new = BETA_VEC * vector_state + (1.0 - BETA_VEC) * vec_grad * vec_grad
-    vec_update = -LEARN_VEC * vec_grad * lax.rsqrt(state_new)
-    terms = terms.reshape(3, nrow_blocks * ncol_blocks, share, BLK).astype(jnp.float32)
-    stats_new = BETA * kron_stats + ((1.0 - BETA) / BLK) * terms[:2]
+    grad_shard, vec_grad, state_new, vec_update, stats_new, update = closing(
+        grad_bf, terms, kron_stats, update, vector_state
+    )
     return (
-        result_back.reshape(1, rows, D),
+        out_back.reshape(1, rows, D),
         dx_back.reshape(1, rows, D),
         grad_shard,
         vec_grad,
         state_new,
         vec_update,
         stats_new,
-        -LEARN * terms[2],
+        update,
     )
 
 

time: 610 us -> 514 us (0.84)
  other arithmetic: 61.3 us -> 27.1 us
  waiting for transfers between devices: 21.1 us -> 0.01 us
  between operations: 14.5 us -> 1.15 us
  starting transfers between devices: 13.4 us -> 1.29 us
  Pallas kernels: 460 us -> 453 us
    pallas_call x1, Pallas kernels: 224 us -> 166 us  [gathered_forward(): pl.pallas_call(forward_kernel, out_shape=(shape((4, D, rows), bf16), shap...]
    pallas_call x1, Pallas kernels: 235 us -> 274 us  [reduced(): pl.pallas_call(functools.partial(reduce_kernel, tuple(edges), scale), out...]
    all_to_all x1 -> x0, waiting for transfers between devices: 21.1 us -> none  [shards(): lax.all_to_all(result_leaving, 'seq', split_axis=0, concat_axis=0, tiled=...]
    convert_element_type x2 -> x1, other arithmetic: 15.4 us -> 2.6 us  [shards(): kron_roots.astype(jnp.bfloat16)]
    pallas_call x0 -> x1, Pallas kernels: none -> 12.6 us  [closing(): pl.pallas_call(closing_kernel, grid=(PARTS,), out_shape=(shape((rows, col...]
    all_to_all x1 -> x0, starting transfers between devices: 12 us -> none  [shards(): lax.all_to_all(result_leaving, 'seq', split_axis=0, concat_axis=0, tiled=...]
    add x1 -> x0, other arithmetic: 6.43 us -> none  [shards(): stats_new = BETA * kron_stats + (1.0 - BETA) / BLK * terms[:2]]
  transfers between devices with their start and end apart: 3 -> 1, of which waited for: 1 -> 0; matrix products, arithmetic and copies ran while one was open for 10% -> 2% of each run, Pallas kernels for 37% -> 0%
where the time goes in v3:
time: 514 us; the launch traced here: 513 us
  Pallas kernels  453 us (88%)
  other arithmetic  27.1 us (5%)
  local copies, waits for them, and re-layouts  17.9 us (3%)
  matrix products  12.7 us (2%)
    pallas_call x1, Pallas kernels, reduced(): pl.pallas_call(functools.partial(reduce_kernel, tuple(edges), scale), out...  274 us
    pallas_call x1, Pallas kernels, gathered_forward(): pl.pallas_call(forward_kernel, out_shape=(shape((4, D, rows), bf16), shap...  166 us
    dot_general x8, matrix products, contract_cols(): lax.dot_general(left, right, (((1,), (1,)), ((), ())), preferred_element_...  12.7 us
    pallas_call x1, Pallas kernels, closing(): pl.pallas_call(closing_kernel, grid=(PARTS,), out_shape=(shape((rows, col...  12.6 us
  transfers between devices with their start and end apart: 1, of which 0 were waited for; matrix products, arithmetic and copies ran while one was open for 2% of the time, Pallas kernels for 0%

profile of v3, /device:TPU:0, one launch (start us, length us, event | category | flops | bytes accessed | tf_op | source)
XLA Modules:
  0.0 512.8 jit_solution(14843971835369179030)
XLA Ops:
  2.6 2.6 convert_element_type.51
  5.2 1.8 copy.30
  8.6 166.4 %gathered_forward.1 = (bf16[4,1024,512]{2,1,0:T(8,128)(2,1)}, bf16[512,1024]{1,0:T(8,128)(2,1)}, bf16[512,1024]{1,0:T(8,128)(2,1)}, f32[512,3072]{1,0:T(8,128)},...) custom-call(s32[8]{0:T(128)} %deal_ref.1, ...), custom_call_target="tpu_custom_call" | custom-call | flops 19327352832 | bytes 100000000 | tf_op jit(solution)/shard_map/gathered_forward/pallas_call | solution.py:1091
  175.0 2.0 multiply_reduce_fusion.3
  177.0 1.6 fusion.5
  178.6 2.3 multiply_reduce_fusion.1
  181.7 1.6 copy-done.13
  184.0 4.0 slice_multiply_fusion.5
  188.0 1.3 collective-permute-start
  190.2 1.3 multiply_convert_fusion.1
  191.5 2.0 fusion.24
  193.5 2.1 fusion.22
  196.6 2.8 gather_fusion
  199.4 2.1 fusion.17
  202.3 4.1 fusion.13
  207.9 1.9 multiply_convert_fusion
  211.1 1.8 pad_maximum_fusion.d_in_ref
  212.8 1.3 copy-done.14
  214.8 1.6 fusion.12
  216.6 2.4 fusion.11
  219.1 1.9 gather_fusion.1
  221.7 273.6 %reduce_chunks.1 = (bf16[256,18176]{1,0:T(8,128)(2,1)}, bf16[2,2,140,16,128]{4,3,2,1,0:T(8,128)(2,1)}, bf16[8,35,16,128]{3,2,1,0:T(8,128)(2,1)}, bf16[8,64,1024]...) custom-call(bf16[4,1024,512]{2,1,0:T(8,128)(2,1)} %get-tuple-element.34.lefts_ref, bf16[512,3072]{1,0:T(8,128)(2,1)} %pad_maximum_fusion.d_in_ref, ...), custom_call_target="tpu_custom_call" | custom-call | flops 18790481920 | bytes 1000000000 | tf_op jit(solution)/shard_map/reduce_chunks/pallas_call | solution.py:642
  495.3 1.6 copy-done
  498.2 12.6 %closing.1 = (f32[256,17920]{1,0:T(8,128)}, f32[5,256]{1,0:T(8,128)}, f32[5,256]{1,0:T(8,128)}, f32[5,256]{1,0:T(8,128)}, f32[2,280,16,128]{3,2,1,0:T(8,128)}, /*index=5*/f32[2,35,4,16,128]{4,3,2,1,0:T(8,128)}) custom-call(bf16[256,18176]{1,0:T(8,128)(2,1)} %get-tuple-element.50.grad_in.vec_in, bf16[256,18176]{1,0:T(8,128)(2,1)} %get-tuple-element.50.grad_in.vec_in, ...), custom_call_target="tpu_custom_call" | custom-call | tf_op jit(solution)/shard_map/closing/pallas_call | solution.py:1191
  (98 shorter events, 15.0 us)
Async XLA Ops:
  5.2 2.7 copy-start.20
  5.2 2.7 copy-start.21
  175.0 3.6 copy-start.19
  175.0 3.6 copy-start.3
  176.9 4.0 copy-start.17
  178.6 2.3 copy-start.8
  178.6 4.6 copy-start.13
  188.0 3.5 copy-start.4
  188.0 3.5 copy-start.6
  188.0 11.4 %collective-permute-start = (f32[2,1024]{1,0:T(2,128)S(1)}, f32[2,1024]{1,0:T(2,128)S(1)}, u32[]{:S(2)}, u32[]{:S(2)}) collective-permute-start(f32[2,1024]{1,0:T(2,128)S(1)} %slice.187), channel_id=1, source_target_pairs={{4,0},{8,4},{12,8},{16,12},{20,16},{24,20},{28,24},{5,1},{9,5},{13... | collective-permute-start | bytes 24584 | tf_op jit(solution)/shard_map/ppermute | solution.py:28
  191.5 4.1 copy-start.11
  193.5 2.1 copy-start.22
  199.4 2.2 copy-start.5
  199.4 2.9 copy-start.7
  199.4 7.0 %slice-start.2 = ((s8[8388608]{0:T(1024)(128)(4,1)}), s8[4194304]{0:T(1024)(128)(4,1)S(1)}, s32[]{:S(2)}) async-start(s8[8388608]{0:T(1024)(128)(4,1)} %bitcast.60), calls=%async_computation.2 | async-start | bytes 8388608
  202.3 4.2 slice-start.3
  211.1 1.8 copy-start.10
  211.1 3.1 copy-start.14
  211.1 3.7 copy-start.15
  214.8 1.9 copy-start.18
  219.0 2.3 copy-start.16
  221.6 273.7 %slice-start = ((s8[4587520]{0:T(1024)(128)(4,1)}), s8[4194304]{0:T(1024)(128)(4,1)S(1)}, s32[]{:S(2)}) async-start(s8[4587520]{0:T(1024)(128)(4,1)} %bitcast.52), calls=%async_computation | async-start | bytes 8388608
  221.7 273.7 %slice-start.1 = ((s8[4587520]{0:T(1024)(128)(4,1)}), s8[393216]{0:T(1024)(128)(4,1)S(1)}, s32[]{:S(2)}) async-start(s8[4587520]{0:T(1024)(128)(4,1)} %bitcast.52), calls=%async_computation.1 | async-start | bytes 786432
  221.7 273.7 %copy-start.2 = (f32[5,256]{1,0:T(8,128)S(1)}, f32[5,256]{1,0:T(8,128)}, u32[]{:S(2)}) copy-start(f32[5,256]{1,0:T(8,128)} %state_in.1) | copy-start | bytes 15364
  (4 other events, 5.7 us)

commit v4 on v3

--- a/solution.py
+++ b/solution.py
@@ -240,15 +240,21 @@
 def reduce_kernel(
     edges,
     scale,
+    inverse_ref,
     lefts_ref,
-    d_in_ref,
-    d_mix_ref,
     d_gu_ref,
     act_ref,
-    vec_ref,
+    smalls_ref,
+    masks_ref,
+    x_ref,
+    dy_ref,
+    proj_ref,
+    prev_ref,
+    h_ref,
+    d_hn_ref,
+    heads_ref,
     owned_ref,
     leave_ref,
-    leave_two_ref,
     grad_ref,
     terms_ref,
     update_ref,
@@ -280,6 +286,20 @@
     own_sem,
     back_send,
     back_recv,
+    x_buf,
+    dy_buf,
+    proj,
+    product_in,
+    h_buf,
+    d_hidden,
+    heads,
+    d_conv,
+    d_proj,
+    d_mix,
+    leave_buf,
+    vec_buf,
+    fetch_sem,
+    halo_sem,
 ):
     z, x, y, c = place()
     seq, wsh = lax.axis_index("seq"), lax.axis_index("wsh")
@@ -300,7 +320,7 @@
     pl.semaphore_wait(barrier, 9)
 
     def far(k, d):
-        source, target = ((leave_ref, arrive_ref), (leave_two_ref, arrive_two_ref))[k]
+        source, target = own_pairs[k]
         to = far_ids[d - 1]
         return pltpu.make_async_remote_copy(
             src_ref=source.at[to[0]],
@@ -311,11 +331,32 @@
             device_id_type=MESH,
         )
 
-    own_pairs = ((leave_ref, arrive_ref), (leave_two_ref, arrive_two_ref))
-    for k, (source, target) in enumerate(own_pairs):
-        pltpu.make_async_copy(source.at[seq], target.at[seq], own_sem.at[k]).start()
-        for d in range(1, 8):
-            far(k, d).start()
+    own_pairs = ((leave_ref, arrive_ref), (leave_buf, arrive_two_ref))
+
+    def own_copy(k):
+        source, target = own_pairs[k]
+        return pltpu.make_async_copy(source.at[seq], target.at[seq], own_sem.at[k])
+
+    own_copy(0).start()
+    for d in range(1, 8):
+        far(0, d).start()
+    fetches = [
+        pltpu.make_async_copy(source, target, fetch_sem.at[k])
+        for k, (source, target) in enumerate(
+            (
+                (h_ref, h_buf),
+                (d_hn_ref, d_hidden),
+                (dy_ref, dy_buf),
+                (proj_ref, proj),
+                (prev_ref, product_in.at[pl.ds(0, 8)]),
+                (heads_ref, heads),
+                (x_ref, x_buf),
+            )
+        )
+    ]
+    for copy in fetches:
+        copy.start()
+    vec_buf[...] = jnp.zeros_like(vec_buf)
 
     batch = update_ref.shape[1] // BATCHES
 
@@ -384,8 +425,8 @@
 
     def b_copies(n):
         slot = lax.rem(n, SEMS)
-        column = n_real - n
-        for r, source in enumerate((d_in_ref, d_mix_ref, d_gu_ref, act_ref)):
+        column = n_real - 1 - n
+        for r, source in enumerate((d_proj, d_mix, d_gu_ref, act_ref)):
             low, high = edges[r], edges[r + 1]
             at = jnp.clip(column - low, 0, high - low - 1)
             at = pl.multiple_of(at * COLS, COLS)
@@ -396,7 +437,7 @@
 
     def r_copies(n):
         slot = lax.rem(n, SEMS)
-        at = jnp.minimum(n_real - n, n_real - 1) // 2
+        at = jnp.maximum(n_real - 1 - n, 0) // 2
         return [
             pltpu.make_async_copy(
                 owned_ref.at[:, kind, at], r_buf.at[slot, kind], r_sem.at[slot, kind]
@@ -405,17 +446,17 @@
         ]
 
     def has_block(n):
-        return (n > 0) & (lax.rem(n_real - n, 2) == lax.rem(seq, 4) // 2)
+        return (n < n_real) & (lax.rem(n_real - 1 - n, 2) == lax.rem(seq, 4) // 2)
 
     def o_copy(n):
-        at = pl.multiple_of((n_real - n) * COLS, COLS)
+        at = pl.multiple_of(lax.rem(2 * n_real - n, n_real + 1) * COLS, COLS)
         return pltpu.make_async_copy(
             final.at[lax.rem(n, RING)], grad_ref.at[:, pl.ds(at, COLS)], o_sem.at[lax.rem(n, SEMS)]
         )
 
     def t_copy(n):
         slot = lax.rem(n, SEMS)
-        at = pl.multiple_of(jnp.minimum(n_real - n, n_real - 1) * 2, 2)
+        at = pl.multiple_of(jnp.maximum(n_real - 1 - n, 0) * 2, 2)
         return pltpu.make_async_copy(
             t_buf.at[slot], terms_ref.at[:, :, pl.ds(at, 2)], t_sem.at[slot]
         )
@@ -438,9 +479,9 @@
 
     def stage_product(n):
         slot = lax.rem(n, RING)
-        column = n_real - n
-
-        @pl.when(n > 0)
+        column = n_real - 1 - n
+
+        @pl.when(n < n_real)
         def _():
             for wanted, copy in b_copies(n):
                 pl.when(wanted)(copy.wait)
@@ -454,10 +495,12 @@
                 )
                 g_buf[slot, w % 2, w // 2] = product.astype(jnp.bfloat16)
 
-        @pl.when(n == 0)
+        @pl.when(n == n_real)
         def _():
             for w in range(4):
-                g_buf[slot, w % 2, w // 2] = vec_ref[w]
+                turned = vec_buf[:, w * 256 : (w + 1) * 256].T.astype(jnp.bfloat16)
+                g_buf[slot, w % 2, w // 2, :, :BLK] = turned
+                g_buf[slot, w % 2, w // 2, :, BLK:] = jnp.zeros_like(turned)
 
         core_copy(n).start()
 
@@ -524,11 +567,11 @@
         slot = lax.rem(n, RING)
         part = lax.rem(n, SEMS)
 
-        @pl.when(n > SEMS)
+        @pl.when(n >= SEMS)
         def _():
             t_copy(n - SEMS).wait()
 
-        @pl.when(n > 0)
+        @pl.when(n < n_real)
         def _():
             picked = lax.broadcasted_iota(jnp.int32, (16, BLK), 1) == (
                 lax.broadcasted_iota(jnp.int32, (16, BLK), 0) + seq * 16
@@ -568,11 +611,11 @@
                 r_buf[part, 1].reshape(BLK, BLK),
                 preferred_element_type=jnp.float32,
             )
-            u_buf[:, (n_real - n) // 2] = both.astype(jnp.bfloat16).reshape(8, 16, BLK)
-
-        column = n_real - n
-
-        @pl.when((n > 0) & (lax.rem(column, 2 * batch) == 0))
+            u_buf[:, (n_real - 1 - n) // 2] = both.astype(jnp.bfloat16).reshape(8, 16, BLK)
+
+        column = n_real - 1 - n
+
+        @pl.when((n < n_real) & (lax.rem(column, 2 * batch) == 0))
         def _():
             b = column // (2 * batch)
             u_own(b).start()
@@ -611,17 +654,143 @@
         ("use", stage_use),
     )
 
+    width = D
+    span = 128
+
+    def gain(k):
+        return smalls_ref[k : k + 1, :].astype(jnp.float32)
+
+    def add_vec(k, value):
+        vec_buf[k : k + 1, :] += jnp.sum(value, axis=0, keepdims=True)
+
+    def shifted(ref, first, by):
+        return ref[first + by : first + by + span]
+
+    def back_norm_two(i):
+        rows = slice(i * span, (i + 1) * span)
+        if i == 0:
+            for copy in fetches[:5]:
+                copy.wait()
+        value, up = h_buf[rows], d_hidden[rows]
+        scale_two = rms_scale(value)
+        scaled = up * gain(1)
+        inner = jnp.mean(scaled * value, axis=1, keepdims=True)
+        add_vec(1, up * value * scale_two)
+        through = scale_two * scaled - value * scale_two * scale_two * scale_two * inner
+        total = wide(dy_buf[rows]) + through
+        d_hidden[rows] = total
+        d_mix[rows] = total.astype(jnp.bfloat16)
+        product_in[8 + i * span : 8 + (i + 1) * span] = (
+            proj[rows, :width] * proj[rows, 2 * width :]
+        )
+
+    def back_out(i):
+        lanes = slice(i * 256, (i + 1) * 256)
+        if i == 0:
+            fetches[5].wait()
+        d_conv[0:512, lanes] = contract_cols(d_mix[:, :HEAD], heads[6, lanes]) + contract_cols(
+            d_mix[:, HEAD:], heads[7, lanes]
+        )
+
+    ring = pltpu.make_async_remote_copy(
+        src_ref=d_conv.at[pl.ds(0, 8)],
+        dst_ref=d_conv.at[pl.ds(512, 8)],
+        send_sem=halo_sem.at[0],
+        recv_sem=halo_sem.at[1],
+        device_id=far_ids[6],
+        device_id_type=MESH,
+    )
+
+    def back_conv(i):
+        rows = slice(i * span, (i + 1) * span)
+        up = d_conv[rows]
+        down = up * proj[rows, width : 2 * width]
+        conv = jnp.zeros_like(up)
+        for k in range(3):
+            term = shifted(product_in, i * span, 6 + k)
+            if k < 2:
+                term = term * masks_ref[k, rows]
+            conv = conv + gain(2 + k) * term
+            add_vec(2 + k, down * term)
+        d_proj[rows, width : 2 * width] = (up * conv).astype(jnp.bfloat16)
+        d_conv[rows] = down
+        if i == 0:
+            ring.start()
+
+    def back_taps(i):
+        rows = slice(i * span, (i + 1) * span)
+        if i == 3:
+            ring.wait()
+            tail = d_conv[512:520]
+            d_conv[512:520] = jnp.where(seq == 7, jnp.zeros_like(tail), tail)
+        first = i * span
+        d_bx = (
+            gain(4) * d_conv[rows]
+            + gain(3) * shifted(masks_ref.at[1], first, 1) * shifted(d_conv, first, 1)
+            + gain(2) * shifted(masks_ref.at[0], first, 2) * shifted(d_conv, first, 2)
+        )
+        d_proj[rows, :width] = (d_bx * proj[rows, 2 * width :]).astype(jnp.bfloat16)
+        d_proj[rows, 2 * width :] = (d_bx * proj[rows, :width]).astype(jnp.bfloat16)
+
+    def back_in(u):
+        part = contract_cols(d_proj[:, u * HEAD : (u + 1) * HEAD], heads[u])
+        if u == 0:
+            h_buf[...] = part
+        else:
+            h_buf[...] += part
+
+    def back_norm_one(i):
+        rows = slice(i * span, (i + 1) * span)
+        if i == 0:
+            fetches[6].wait()
+        value = jnp.concatenate([wide(x_buf[2 * i]), wide(x_buf[2 * i + 1])], axis=0)
+        up = h_buf[rows]
+        scale_one = rms_scale(value)
+        scaled = up * gain(0)
+        inner = jnp.mean(scaled * value, axis=1, keepdims=True)
+        add_vec(0, up * value * scale_one)
+        through = scale_one * scaled - value * scale_one * scale_one * scale_one * inner
+        total = (d_hidden[rows] + through).astype(jnp.bfloat16)
+        x_buf[2 * i] = total[:64]
+        x_buf[2 * i + 1] = total[64:]
+
+    def back_pick(i):
+        for d in range(4 * i, 4 * i + 4):
+            leave_buf[d] = x_buf[inverse_ref[d]]
+
+    def back_leave(i):
+        if i == 0:
+            own_copy(1).start()
+        far(1, i + 1).start()
+
+    pieces = []
+    for work, number, pause in (
+        (back_norm_two, 4, 3),
+        (back_out, 4, 0),
+        (back_conv, 4, 0),
+        (back_taps, 4, 4),
+        (back_in, 6, 0),
+        (back_norm_one, 4, 0),
+        (back_pick, 2, 0),
+        (back_leave, 7, 0),
+    ):
+        pieces.extend([None] * pause)
+        pieces.extend(functools.partial(work, i) for i in range(number))
+
     def step(t, carry):
         for name, stage in stages:
             n = t - offsets[name]
             pl.when((n >= 0) & (n < count))(functools.partial(stage, n))
+        for at, piece in enumerate(pieces):
+            if piece is not None:
+                pl.when(t == at)(piece)
         return carry
 
     lax.fori_loop(0, count + offsets["done"], step, 0)
-    for n in range(count - SEMS, count):
+    for n in range(count - SEMS, n_real):
         t_copy(n).wait()
-    for k, (source, target) in enumerate(own_pairs):
-        pltpu.make_async_copy(source.at[seq], target.at[seq], own_sem.at[k]).wait()
+    for k in range(2):
+        own_copy(k).wait()
         for d in range(1, 8):
             far(k, d).wait()
     for b in range(BATCHES):
@@ -630,13 +799,13 @@
             u_back(b, d).wait()
 
 
-def reduced(lefts, rights, vec, owned, leaving, scale):
+def reduced(inverse, lefts, d_gu, act, smalls, masks, mixer, owned, leaving, scale):
     edges = [0]
-    for right in rights:
-        edges.append(edges[-1] + right.shape[1] // COLS)
-    rows = rights[0].shape[0]
+    for columns in (3 * D, D, d_gu.shape[1], act.shape[1]):
+        edges.append(edges[-1] + columns // COLS)
+    rows = act.shape[0]
     count = edges[-1]
-    bf16 = jnp.bfloat16
+    bf16, f32 = jnp.bfloat16, jnp.float32
     anywhere = pl.BlockSpec(memory_space=pl.ANY)
     vmem = pl.BlockSpec(memory_space=pltpu.VMEM)
     return pl.pallas_call(
@@ -645,10 +814,18 @@
             jax.ShapeDtypeStruct((256, (count + 1) * COLS), bf16),
             jax.ShapeDtypeStruct((2, 2, count * 2, 16, BLK), bf16),
             jax.ShapeDtypeStruct((8, count // 2, 16, BLK), bf16),
-            jax.ShapeDtypeStruct(leaving[0].shape, bf16),
-            jax.ShapeDtypeStruct(leaving[1].shape, bf16),
+            jax.ShapeDtypeStruct(leaving.shape, bf16),
+            jax.ShapeDtypeStruct(leaving.shape, bf16),
         ),
-        in_specs=[vmem, anywhere, anywhere, anywhere, anywhere, vmem, anywhere, anywhere, anywhere],
+        in_specs=[
+            pl.BlockSpec(memory_space=pltpu.SMEM),
+            vmem,
+            anywhere,
+            anywhere,
+            vmem,
+            vmem,
+        ]
+        + [anywhere] * 9,
         out_specs=(anywhere,) * 5,
         scratch_shapes=[
             pltpu.VMEM((SEMS, rows, COLS), bf16),
@@ -677,15 +854,29 @@
             pltpu.SemaphoreType.DMA((2 + BATCHES,)),
             pltpu.SemaphoreType.DMA((BATCHES, 7)),
             pltpu.SemaphoreType.DMA((BATCHES, 7)),
+            pltpu.VMEM(leaving.shape, bf16),
+            pltpu.VMEM((rows, D), bf16),
+            pltpu.VMEM((rows, 3 * D), f32),
+            pltpu.VMEM((rows + 8, D), f32),
+            pltpu.VMEM((rows, D), f32),
+            pltpu.VMEM((rows, D), f32),
+            pltpu.VMEM((8, D, HEAD), bf16),
+            pltpu.VMEM((rows + 8, D), f32),
+            pltpu.VMEM((rows, 3 * D), bf16),
+            pltpu.VMEM((rows, D), bf16),
+            pltpu.VMEM(leaving.shape, bf16),
+            pltpu.VMEM((BLK, D), f32),
+            pltpu.SemaphoreType.DMA((7,)),
+            pltpu.SemaphoreType.DMA((2,)),
         ],
         compiler_params=pltpu.CompilerParams(
-            collective_id=0, has_side_effects=True, vmem_limit_bytes=48 << 20
+            collective_id=0, has_side_effects=True, vmem_limit_bytes=62 << 20
         ),
         cost_estimate=pl.CostEstimate(
             flops=2 * rows * 1024 * count * COLS, bytes_accessed=10**9, transcendentals=0
         ),
         name="reduce_chunks",
-    )(lefts, *rights, vec, owned, *leaving)
+    )(inverse, lefts, d_gu, act, smalls, masks, *mixer, owned, leaving)
 
 
 HEAD = 512
@@ -694,6 +885,7 @@
 
 def forward_kernel(
     deal_ref,
+    inverse_ref,
     tokens_ref,
     dy_ref,
     weights_ref,
@@ -1055,9 +1247,12 @@
     turn(hn, 2, True)
     out_back = pltpu.make_async_copy(back.at[pl.ds(0, 512)], d_hn_ref, out_sem.at[3])
     out_back.start()
-    yc[...] = total[...].astype(bf16)
+    for k in range(8):
+        x_in[k] = total[k * 64 : (k + 1) * 64].astype(bf16)
+    for k in range(8):
+        dy_in[k] = x_in[inverse_ref[k]]
     last = (
-        pltpu.make_async_copy(yc, result_ref, out_sem.at[4]),
+        pltpu.make_async_copy(dy_in, result_ref, out_sem.at[4]),
         pltpu.make_async_copy(xs, x_ref, out_sem.at[5]),
         pltpu.make_async_copy(dys, dy_out_ref, out_sem.at[6]),
         pltpu.make_async_copy(smalls, smalls_ref, out_sem.at[7]),
@@ -1079,7 +1274,7 @@
     pltpu.make_async_copy(turned, lefts_ref.at[2], out_sem.at[0]).wait()
 
 
-def gathered_forward(deal_order, tokens, dys, weights, small, masks, roots):
+def gathered_forward(deal_order, inverse, tokens, dys, weights, small, masks, roots):
     bf16, f32 = jnp.bfloat16, jnp.float32
     rows = tokens.shape[0] * tokens.shape[1]
     n_heads = 4 * D // HEAD
@@ -1100,12 +1295,13 @@
             shape((rows, FF), bf16),
             shape((rows, 2 * FF), bf16),
             shape((rows, D), f32),
-            shape((rows, D), bf16),
+            shape(tokens.shape, bf16),
             shape((n_heads, D, HEAD), bf16),
             shape((8, D), bf16),
             shape(roots.shape, bf16),
         ),
         in_specs=[
+            pl.BlockSpec(memory_space=pltpu.SMEM),
             pl.BlockSpec(memory_space=pltpu.SMEM),
             anywhere,
             anywhere,
@@ -1152,7 +1348,7 @@
             flops=8 * rows * D * FF, bytes_accessed=10**8, transcendentals=0
         ),
         name="gathered_forward",
-    )(deal_order, tokens, dys, weights, small, masks, roots)
+    )(deal_order, inverse, tokens, dys, weights, small, masks, roots)
 
 
 PARTS = 7
@@ -1228,12 +1424,6 @@
     return (*outs[:5], outs[5].reshape(blocks, share, BLK))
 
 
-def contract_units(left, units):
-    return sum(
-        contract_cols(left[:, u * HEAD : (u + 1) * HEAD], units[u]) for u in range(units.shape[0])
-    )
-
-
 def shards(
     tokens_in,
     out_grad,
@@ -1251,8 +1441,12 @@
     rows = tokens_in.shape[1]
     unit = rows // n_seq
     first_row = lax.axis_index("seq") * rows
-    pos = seq_positions(seq_lengths[0], first_row, rows + 2)
-    masks = [(pos >= 2 - k).astype(jnp.float32)[:, None] for k in range(3)]
+    pos = seq_positions(seq_lengths[0], first_row, rows + 8)
+    masks = jnp.stack([(pos >= 2 - k).astype(jnp.float32)[:, None] for k in range(2)])
+    classes = jnp.arange(n_seq, dtype=jnp.int32)
+    inverse = jnp.sum(
+        jnp.where(deal_order[None, :] == classes[:, None], classes[None, :], 0), axis=1
+    )
     nrow_blocks, ncol_blocks = weights.shape[0] // BLK, weights.shape[1] // BLK
     share = BLK // n_seq
     roots = kron_roots.astype(jnp.bfloat16).reshape(
@@ -1278,57 +1472,24 @@
         owned,
     ) = gathered_forward(
         deal_order,
+        inverse,
         tokens_in.reshape(n_seq, unit, D),
         out_grad.reshape(n_seq, unit, D),
         weights,
         small,
-        jnp.stack([masks[0][:rows], masks[1][:rows]]),
+        masks,
         roots,
     )
-    gains = smalls[:2].astype(jnp.float32)
-    kernel = smalls[2:5].astype(jnp.float32)
-    xf = x_bf.astype(jnp.float32)
-    scale_one = rms_scale(xf)
-    scale_two = rms_scale(hidden_sum)
-    b_part = proj[:, :D]
-    c_part = proj[:, D : 2 * D]
-    x_part = proj[:, 2 * D :]
-    ext = jnp.concatenate([prev[6:], b_part * x_part], axis=0)
-    conv = (
-        kernel[0] * masks[0][:rows] * ext[0:rows]
-        + kernel[1] * masks[1][:rows] * ext[1 : rows + 1]
-        + kernel[2] * masks[2][:rows] * ext[2 : rows + 2]
-    )
-    d_norm_two, g_gain_two = norm_back(d_hn, hidden_sum, scale_two, gains[1])
-    d_hidden = dy_bf.astype(jnp.float32) + d_norm_two
-    d_mix = d_hidden.astype(jnp.bfloat16)
-    d_yc = contract_units(d_mix, heads[3 * D // HEAD :])
-    d_c = d_yc * conv
-    d_conv = d_yc * c_part
-    after = passed_along(d_conv[:2], "seq", -1)
-    d_ext = jnp.concatenate([d_conv, after], axis=0)
-    weighted = [d_ext * masks[k] for k in range(3)]
-    d_bx = (
-        kernel[2] * weighted[2][:rows]
-        + kernel[1] * weighted[1][1 : rows + 1]
-        + kernel[0] * weighted[0][2 : rows + 2]
-    )
-    g_taps = jnp.stack([jnp.sum(weighted[k][:rows] * ext[k : k + rows], axis=0) for k in range(3)])
-    d_proj = jnp.concatenate([d_bx * x_part, d_c, d_bx * b_part], axis=1).astype(jnp.bfloat16)
-    d_xn = contract_units(d_proj, heads[: 3 * D // HEAD])
-    d_norm_one, g_gain_one = norm_back(d_xn, xf, scale_one, gains[0])
-    d_input = (d_hidden + d_norm_one).astype(jnp.bfloat16)
-    g_vec = jnp.concatenate([g_gain_one[None], g_gain_two[None], g_taps], axis=0)
-    inverse = jnp.argsort(deal_order)
-    result_leaving = jnp.take(result.reshape(n_seq, unit, D), inverse, axis=0)
-    leaving = jnp.take(d_input.reshape(n_seq, unit, D), inverse, axis=0)
-    vec = jnp.pad(g_vec.T.astype(jnp.bfloat16), ((0, 0), (0, COLS - g_vec.shape[0])))
     grad_bf, terms, update, out_back, dx_back = reduced(
+        inverse,
         lefts,
-        (d_proj, d_mix, d_gu, act),
-        vec.reshape(n_wsh, D // n_wsh, COLS),
+        d_gu,
+        act,
+        smalls,
+        masks,
+        (x_bf.reshape(n_seq, unit, D), dy_bf, proj, prev, hidden_sum, d_hn, heads),
         owned,
-        (result_leaving, leaving),
+        result,
         float((rows * n_seq * n_wsh) ** -0.5),
     )
     grad_shard, vec_grad, state_new, vec_update, stats_new, update = closing(

time: 514 us -> 468 us (0.911)
  other arithmetic: 27.1 us -> 7.81 us
  matrix products: 12.7 us -> 0 us
  local copies, waits for them, and re-layouts: 17.9 us -> 9.01 us
    dot_general x8 -> x0, matrix products: 12.7 us -> none  [contract_cols(): lax.dot_general(left, right, (((1,), (1,)), ((), ())), preferred_element_...]
    reduce_sum x4 -> x1, other arithmetic: 9.97 us -> 1.28 us  [shards(): jnp.sum(jnp.where(deal_order[None, :] == classes[:, None], classes[None,...]
  transfers between devices with their start and end apart: 1 -> 0, of which waited for: 0 -> 0; matrix products, arithmetic and copies ran while one was open for 2% -> 0% of each run, Pallas kernels for 0% -> 0%
where the time goes in v4:
time: 468 us
  Pallas kernels  450 us (96%)
  local copies, waits for them, and re-layouts  9.01 us (2%)
  other arithmetic  7.81 us (2%)
    pallas_call x1, Pallas kernels, reduced(): pl.pallas_call(functools.partial(reduce_kernel, tuple(edges), scale), out...  271 us
    pallas_call x1, Pallas kernels, gathered_forward(): pl.pallas_call(forward_kernel, out_shape=(shape((4, D, rows), bf16), shap...  166 us
    pallas_call x1, Pallas kernels, closing(): pl.pallas_call(closing_kernel, grid=(PARTS,), out_shape=(shape((rows, col...  12.8 us

profile of v4, /device:TPU:0, one launch (start us, length us, event | category | flops | bytes accessed | tf_op | source)
XLA Modules:
  0.0 467.8 jit_solution(11558023022844180732)
XLA Ops:
  0.6 1.3 select_reduce_fusion.1.inverse_ref
  1.9 0.8 reduce-window_clone.1
  2.7 0.7 subtract_bitcast_fusion
  3.4 0.1 pad.4.clone
  3.5 1.4 maximum_maximum_fusion.small_ref
  4.8 0.1 select_reduce_fusion
  4.9 0.1 fusion.1
  5.1 0.9 add_convert_fusion.masks_ref
  5.9 2.6 convert_element_type.19
  8.5 1.8 copy.29
  10.3 166.4 %gathered_forward.1 = (bf16[4,1024,512]{2,1,0:T(8,128)(2,1)}, bf16[512,1024]{1,0:T(8,128)(2,1)}, bf16[512,1024]{1,0:T(8,128)(2,1)}, f32[512,3072]{1,0:T(8,128)},...) custom-call(s32[8]{0:T(128)} %deal_ref.1, ...), custom_call_target="tpu_custom_call" | custom-call | flops 19327352832 | bytes 100000000 | tf_op jit(solution)/shard_map/gathered_forward/pallas_call | solution.py:1286
  176.7 0.0 copy-start.3
  176.7 271.1 %reduce_chunks.1 = (bf16[256,18176]{1,0:T(8,128)(2,1)}, bf16[2,2,140,16,128]{4,3,2,1,0:T(8,128)(2,1)}, bf16[8,35,16,128]{3,2,1,0:T(8,128)(2,1)}, bf16[8,64,1024]{2,1,0:T(8,128)(2,1)}, bf16[8,64,1024]{2,1,0:T(8,128)(2,1)}) custom-call(s32[8]{0:T(128)} %select_reduce_fusion.1.inverse_ref, bf16[4,1024,512]{2,1,0:T(8,128)(2,1)} %get-tuple-element.32.lefts_ref, ...), custom_call_target="tpu_custom_call" | custom-call | flops 18790481920 | bytes 1000000000 | tf_op jit(solution)/shard_map/reduce_chunks/pallas_call | solution.py:811
  447.8 0.0 copy-done.3
  447.8 0.0 copy-start
  447.8 2.3 copy-done
  450.1 0.0 copy-start.1
  450.1 1.6 copy-done.1
  451.8 1.3 copy-done.2
  453.0 12.8 %closing.1 = (f32[256,17920]{1,0:T(8,128)}, f32[5,256]{1,0:T(8,128)}, f32[5,256]{1,0:T(8,128)}, f32[5,256]{1,0:T(8,128)}, f32[2,280,16,128]{3,2,1,0:T(8,128)}, /*index=5*/f32[2,35,4,16,128]{4,3,2,1,0:T(8,128)}) custom-call(bf16[256,18176]{1,0:T(8,128)(2,1)} %get-tuple-element.47.grad_in.vec_in, bf16[256,18176]{1,0:T(8,128)(2,1)} %get-tuple-element.47.grad_in.vec_in, ...), custom_call_target="tpu_custom_call" | custom-call | tf_op jit(solution)/shard_map/closing/pallas_call | solution.py:1387
  465.8 0.0 copy-done.5
  465.8 1.0 copy.32
  466.8 0.0 copy-done.4
  466.8 1.0 copy.33
  (5 shorter events, 0.0 us)
Async XLA Ops:
  176.7 271.1 %copy-start.3 = (f32[5,256]{1,0:T(8,128)S(1)}, f32[5,256]{1,0:T(8,128)}, u32[]{:S(2)}) copy-start(f32[5,256]{1,0:T(8,128)} %state_in.1) | copy-start | bytes 15364
  447.8 2.3 copy-start
  450.1 1.6 copy-start.1
  451.8 1.3 copy-start.2
  453.0 12.8 %copy-start.5 = (bf16[8,64,1024]{2,1,0:T(8,128)(2,1)S(1)}, bf16[8,64,1024]{2,1,0:T(8,128)(2,1)}, u32[]{:S(2)}) copy-start(bf16[8,64,1024]{2,1,0:T(8,128)(2,1)} %get-tuple-element.45) | copy-start | bytes 3145732
  453.0 13.7 %copy-start.4 = (bf16[8,64,1024]{2,1,0:T(8,128)(2,1)S(1)}, bf16[8,64,1024]{2,1,0:T(8,128)(2,1)}, u32[]{:S(2)}) copy-start(bf16[8,64,1024]{2,1,0:T(8,128)(2,1)} %get-tuple-element.46) | copy-start | bytes 3145732
